TPU v7x, 32 devices: a whole 2x2x4 slice. The times are simulated.
32 devices in a mesh: gx: 8 (over z, y), gy: 4 (over x, core).
Axes of the slice: x: 2, y: 2, z: 4, core: 2. Of those that a mesh axis runs over, the one named last changes fastest.
Arguments:
- block_list: int32 [64], P(('gx', 'gy')), may hold values from -1 to 63, as said below
- wet_levels: int32 [64, 1800], P(('gx', 'gy')), may hold values from 0 to 62, as said below
- mixing: float32 [64, 1800], P(('gx', 'gy')), may hold values from 0.5 to 2
- velocity: float32 [64, 2, 62, 1800], P(('gx', 'gy')), may hold values from -3 to 3
- tracers: float32 [64, 2, 62, 1800], P(('gx', 'gy')), may hold values from -6 to 6
- damping: float32 [160, 720], P('gy', 'gx'), may hold values from 0.05 to 0.5
Outputs:
- new_tracers: float32 [64, 2, 62, 1800], P(('gx', 'gy'))
- surface_height: float32 [160, 720], P('gy', 'gx')
Inputs may be any that keep to these rules, and one draw needn't show every extreme that they name: `block_list`: slots form runs of 2 (run j holds slots j * 2 to j * 2 + 1). With q = j // 4 and r = j % 4, run j names distinct blocks r * 16 + q * 2 + s with 0 <= s < 2, in any order, and -1 in its remaining slots. Every run names one block or more, and the last run names all 2. Blocks that no run names are land. `wet_levels`: 0 in every slot whose block_list entry is -1; some column has 62 wet levels.
All inputs are finite; a program needn't handle non-finite values.
Results may differ from a plain program's by a relative error of at most 0.0003.
Values sent between devices are 32-bit elements; how exact they have to be, the bound alone decides.
A program may use at most 128 MiB of HBM per device.

v0:
```python
import math

import jax
import jax.numpy as jnp
from jax import lax
from jax.sharding import PartitionSpec as P

BX = 45
BY = 40
PASSES = 2
ITERS = 3


advect_rate = 0.25
mixing_rate = 0.015
salt_weight = 0.8
directions = ((0, 1), (0, -1), (1, 0), (-1, 0))


def with_halo(cells, sides, width):
    for axis, dim in sides:
        count = lax.axis_size(axis)
        head = lax.slice_in_dim(cells, 0, width, axis=dim)
        tail = lax.slice_in_dim(cells, cells.shape[dim] - width, cells.shape[dim], axis=dim)
        cells = jnp.concatenate(
            [
                lax.ppermute(tail, axis, [(i, (i + 1) % count) for i in range(count)]),
                cells,
                lax.ppermute(head, axis, [((i + 1) % count, i) for i in range(count)]),
            ],
            axis=dim,
        )
    return cells


def window(values, shrink, step_y, step_x):
    height = values.shape[-2]
    breadth = values.shape[-1]
    return values[
        ..., shrink + step_y : height - shrink + step_y, shrink + step_x : breadth - shrink + step_x
    ]


def laplace(values, wetness, shrink):
    centre = window(values, shrink, 0, 0)
    wet_centre = window(wetness, shrink, 0, 0)
    pieces = [
        wet_centre
        * window(wetness, shrink, step_y, step_x)
        * (window(values, shrink, step_y, step_x) - centre)
        for step_y, step_x in directions
    ]
    return pieces[0] + pieces[1] + pieces[2] + pieces[3]


def advect(values, wetness, eastward, northward):
    centre = window(values, 2, 0, 0)
    wet_centre = window(wetness, 2, 0, 0)

    def face_flux(speeds, step_y, step_x):
        face_speed = 0.5 * (window(speeds, 2, 0, 0) + window(speeds, 2, step_y, step_x))
        face_wet = wet_centre * window(wetness, 2, step_y, step_x)
        return face_wet * face_speed * (0.5 * (centre + window(values, 2, step_y, step_x)))

    return -(
        face_flux(eastward, 0, 1)
        - face_flux(eastward, 0, -1)
        + face_flux(northward, 1, 0)
        - face_flux(northward, -1, 0)
    )


def tracer_pass(padded, wetness, eastward, northward, mixing):
    first_lap = laplace(padded, wetness, 1)
    scaled = window(mixing, 1, 0, 0) * first_lap
    biharmonic = -laplace(scaled, window(wetness, 1, 0, 0), 1)
    return (
        window(padded, 2, 0, 0)
        + advect_rate * advect(padded, wetness, eastward, northward)
        + mixing_rate * biharmonic
    )


def to_strip(slot_values, selector):
    placed = jnp.einsum("ps,s...->p...", selector, slot_values, precision=lax.Precision.HIGHEST)
    slot_count = placed.shape[0]
    middle = placed.shape[1:-1]
    leading = len(middle)
    placed = placed.reshape((slot_count,) + middle + (BY, BX))
    axes_order = tuple(range(1, leading + 1)) + (leading + 1, 0, leading + 2)
    return placed.transpose(axes_order).reshape(middle + (BY, slot_count * BX))


def from_strip(strip_values, selector):
    slot_count = selector.shape[0]
    middle = strip_values.shape[:-2]
    leading = len(middle)
    blocks = strip_values.reshape(middle + (BY, slot_count, BX))
    axes_order = (leading + 1,) + tuple(range(leading)) + (leading, leading + 2)
    blocks = blocks.transpose(axes_order).reshape((slot_count,) + middle + (BY * BX,))
    return jnp.einsum("ps,p...->s...", selector, blocks, precision=lax.Precision.HIGHEST)


def per_device(block_list, wet_levels, mixing, velocity, tracers, damping):
    slot_count = block_list.shape[0]
    level_numbers = tracers.shape[2]
    present = block_list >= 0
    position = jnp.where(present, block_list % slot_count, -1)
    selector = (position[None, :] == jnp.arange(slot_count, dtype=jnp.int32)[:, None]).astype(
        jnp.float32
    )
    margin = 2
    flow_strip = to_strip(velocity, selector)
    flow_strip = flow_strip.reshape((2 * level_numbers,) + flow_strip.shape[2:])
    depth_strip = to_strip(wet_levels.astype(jnp.float32), selector)
    mixing_strip = to_strip(mixing, selector)
    static = jnp.concatenate([flow_strip, depth_strip[None], mixing_strip[None]], axis=0)
    padded_static = with_halo(static, (("gx", 2), ("gy", 1)), margin)
    row_index = lax.broadcasted_iota(jnp.int32, padded_static.shape[1:], 0)
    row_total = padded_static.shape[1]
    row_owner = lax.axis_index("gy")
    outside = (row_owner == 0) & (row_index < margin) | (row_owner == lax.axis_size("gy") - 1) & (
        row_index >= row_total - margin
    )
    depth_pad = jnp.where(outside, 0.0, padded_static[-2])
    mixing_pad = padded_static[-1]
    east_pad = padded_static[:level_numbers]
    north_pad = padded_static[level_numbers : 2 * level_numbers]
    current = to_strip(tracers, selector)
    for pass_index in range(PASSES):
        padded = with_halo(current, (("gx", 3), ("gy", 2)), margin)
        eastward = window(east_pad, 0, 0, 0)
        northward = window(north_pad, 0, 0, 0)
        depth_now = window(depth_pad, 0, 0, 0)
        mixing_now = window(mixing_pad, 0, 0, 0)
        advance_level_ids = lax.broadcasted_iota(jnp.int32, (level_numbers, 1, 1), 0)
        wetness = (advance_level_ids.astype(jnp.float32) < depth_now[None]).astype(jnp.float32)
        current = tracer_pass(padded, wetness, eastward, northward, mixing_now)
    inner_depth = window(depth_pad, margin, 0, 0)
    level_ids = lax.broadcasted_iota(jnp.int32, (level_numbers, 1, 1), 0)
    wet_inner = (level_ids.astype(jnp.float32) < inner_depth[None]).astype(jnp.float32)
    forcing = jnp.sum(wet_inner * (current[0] - salt_weight * current[1]), axis=0) / math.sqrt(
        level_numbers
    )
    height_pad = window(depth_pad, margin - 1, 0, 0)
    centre_depth = window(height_pad, 1, 0, 0)
    couplings = [
        jnp.minimum(centre_depth, window(height_pad, 1, step_y, step_x)) / level_numbers
        for step_y, step_x in directions
    ]
    diagonal = damping + (couplings[0] + couplings[1] + couplings[2] + couplings[3])

    def operate(values):
        padded = with_halo(values, (("gx", 1), ("gy", 0)), 1)
        beside = [
            couplings[number] * window(padded, 1, step_y, step_x)
            for number, (step_y, step_x) in enumerate(directions)
        ]
        return diagonal * values - (beside[0] + beside[1] + beside[2] + beside[3])

    def two_products(residual, applied):
        return lax.psum((jnp.sum(residual * residual), jnp.sum(residual * applied)), ("gx", "gy"))

    solution = jnp.zeros_like(forcing)
    residual = forcing
    applied = operate(residual)
    norm_now, product = two_products(residual, applied)
    step_size = norm_now / product
    direction = residual
    carried = applied
    for iteration in range(ITERS):
        solution = solution + step_size * direction
        residual = residual - step_size * carried
        if iteration + 1 < ITERS:
            applied = operate(residual)
            norm_next, product = two_products(residual, applied)
            growth = norm_next / norm_now
            step_size = norm_next / (product - growth * norm_next / step_size)
            direction = residual + growth * direction
            carried = applied + growth * carried
            norm_now = norm_next
    restored = from_strip(current, selector)
    new_tracers = jnp.where(present[:, None, None, None], restored, tracers)
    return (new_tracers, solution)


def solution(mesh):
    return jax.shard_map(
        per_device,
        mesh=mesh,
        in_specs=(
            P(("gx", "gy")),
            P(("gx", "gy"), None),
            P(("gx", "gy"), None),
            P(("gx", "gy"), None, None, None),
            P(("gx", "gy"), None, None, None),
            P("gy", "gx"),
        ),
        out_specs=(P(("gx", "gy"), None, None, None), P("gy", "gx")),
        check_vma=False,
    )
```

profile of v0, /device:TPU:0, one launch (start us, length us, event | category | flops | bytes accessed | tf_op | source)
XLA Modules:
  0.0 371.8 jit_solution(12722090164968238049)
XLA Ops:
  1.4 6.8 %fusion.82 = f32[2,2,62,1800]{3,0,2,1:T(2,128)S(1)} fusion(f32[2,2,62,1800]{3,1,2,0:T(2,128)} %param.10, s32[2]{0:T(128)S(1)} %fusion.120), kind=kOutput, calls=%fused_computation.140 | convolution fusion | flops 10713604 | bytes 3571208 | tf_op jit(solution)/shard_map/ps,s...->p.../dot_general | solution.py:85
  8.3 1.4 copy.154
  9.7 5.0 %reshape.59 = f32[2,2,62,40,45]{4,3,2,1,0:T(8,128)} reshape(f32[2,2,62,1800]{3,2,1,0:T(8,128)} %copy.154) | data formatting | bytes 3571200 | tf_op jit(solution)/shard_map/reshape | solution.py:89
  14.7 5.8 %copy.155 = f32[2,62,40,2,45]{1,2,4,3,0:T(8,128)} copy(f32[2,62,40,2,45]{4,2,1,0,3:T(8,128)} %bitcast.57) | data formatting | bytes 3571200 | tf_op jit(solution)/shard_map/transpose | solution.py:91
  20.5 0.9 fusion.131
  21.5 3.0 collective-permute-start.5
  24.5 3.3 collective-permute-start
  28.9 2.0 copy.162
  30.8 1.9 copy.163
  32.8 5.1 %fusion.60 = f32[2,2,62,1800]{3,0,2,1:T(2,128)S(1)} fusion(f32[2,2,62,1800]{3,1,2,0:T(2,128)S(1)} %copy-done, s32[2]{0:T(128)S(1)} %fusion.120), kind=kOutput, calls=%fused_computation.97 | convolution fusion | flops 10713604 | bytes 3571208 | tf_op jit(solution)/shard_map/ps,s...->p.../dot_general | solution.py:85
  37.8 1.5 copy.158
  39.3 5.1 %reshape.61 = f32[2,2,62,40,45]{4,3,2,1,0:T(8,128)} reshape(f32[2,2,62,1800]{3,2,1,0:T(8,128)} %copy.158) | data formatting | bytes 3571200 | tf_op jit(solution)/shard_map/reshape | solution.py:89
  44.4 8.7 %copy.159 = f32[2,62,40,2,45]{1,0,2,4,3:T(2,128)} copy(f32[2,62,40,2,45]{4,2,1,0,3:T(8,128)} %bitcast.54) | data formatting | bytes 3571200 | tf_op jit(solution)/shard_map/transpose | solution.py:91
  53.1 5.0 %reshape_reshape.3 = f32[124,40,90]{0,1,2:T(8,128)} reshape(f32[2,62,40,2,45]{1,0,2,4,3:T(2,128)} %copy.159) | data formatting | bytes 3571200 | tf_op jit(solution)/shard_map/reshape;reshape | solution.py:114
  58.1 1.1 pad_maximum_fusion.65
  59.3 4.7 %collective-permute-start.2 = (f32[126,40,2]{0,1,2:T(8,128)S(1)}, f32[126,40,2]{0,1,2:T(8,128)S(1)}, u32[]{:S(2)}, u32[]{:S(2)}) collective-permute-start(f32[126,40,2]{0,1,2:T(8,128)S(1)} %get-tuple-element.43), channel_id=1, source_target_pairs={{4,0},{8,4},{12,8},{16,12},{20,16},{24,20},{28,24},{0,28},{5,1},{9... | collective-permute-start | bytes 120968 | tf_op jit(solution)/shard_map/ppermute | solution.py:29
  64.0 2.7 fusion.129
  66.6 3.3 copy.166
  69.9 3.3 copy.167
  73.2 1.7 pad_maximum_fusion.30
  76.2 1.1 collective-permute-start.3
  77.3 0.9 collective-permute-start.4
  78.2 1.1 collective-permute-done.6
  79.3 2.8 collective-permute-done.7
  82.2 4.1 %pad_maximum_fusion = (f32[2,62,42,94]{1,2,3,0:T(8,128)}, f32[2,62,42,94]{1,2,3,0:T(8,128)}) fusion(f32[2,62,2,94]{1,2,3,0:T(2,128)S(1)} %collective-permute-done.6, f32[2,62,40,2]{1,2,3,0:T(8,128)S(1)} %collective-permute-done, f32[2,62,40,90]{1,2,3,0:T(8,128)S(1)} %bitcast.52, f32[2,62,40,2]{1,2,3,0:T(8,128)S(1)} %collective-permute-done.5, ...), kind=kLoop, calls=%fused_computation | loop fusion | flops 2937312 | bytes 5967872 | tf_op jit(solution)/shard_map/concatenate | solution.py:25
  86.3 2.7 pad_maximum_fusion.1
  89.0 1.2 pad_maximum_fusion.8
  90.3 4.2 %fusion.132 = (f32[1,44,94]{0,1,2:T(8,128)}, f32[1,44,94]{0,1,2:T(8,128)}, f32[1,44,94]{0,1,2:T(8,128)}) fusion(f32[126,44,94]{0,1,2:T(8,128)S(1)} %pad_maximum_fusion.8, pred[44]{0:T(512)(128)(4,1)S(1)} %and_or_fusion), kind=kLoop, calls=%fused_computation.254 | loop fusion | flops 4136 | bytes 82764 | tf_op jit(solution)/shard_map/slice | solution.py:125
  94.5 2.5 copy.168
  97.2 2.5 copy.183
  100.4 3.9 %slice_multiply_fusion.3 = (f32[62,42,92]{0,1,2:T(8,128)}, f32[62,42,92]{0,1,2:T(8,128)}, f32[62,42,92]{0,1,2:T(8,128)}, f32[62,42,92]{0,1,2:T(8,128)}) fusion(f32[62,44,94]{0,1,2:T(8,128)S(1)} %compare_convert_fusion), kind=kLoop, calls=%fused_computation.96 | loop fusion | flops 958272 | bytes 8624448 | tf_op jit(solution)/shard_map/mul | solution.py:48
  104.3 12.2 %fusion.10 = f32[2,62,42,92]{1,2,3,0:T(8,128)S(1)} fusion(f32[2,62,42,94]{1,2,3,0:T(8,128)} %get-tuple-element.51, f32[2,62,42,94]{1,2,3,0:T(8,128)} %get-tuple-element.50, f32[2,62,44,94]{1,2,3,0:T(8,128)} %pad_maximum_fusion.1, f32[62,42,92]{0,1,2:T(8,128)} %get-tuple-element.63, f32[62,42,92]{0,1,2:T(8,128)} %get-tuple-element.64, ...), kind=kLoop, calls=%fused_computation.21 | loop fusion | flops 5749632 | bytes 15347808 | tf_op jit(solution)/shard_map/mul | solution.py:75
  116.5 7.8 %fusion.73 = (f32[62,40,90]{0,1,2:T(8,128)}, f32[62,40,90]{0,1,2:T(8,128)}, f32[62,40,90]{0,1,2:T(8,128)}, f32[62,40,90]{0,1,2:T(8,128)}) fusion(f32[126,2,94]{0,1,2:T(2,128)S(1)} %collective-permute-done.4, f32[126,40,2]{0,1,2:T(8,128)S(1)} %collective-permute-done.2, f32[126,40,2]{0,1,2:T(8,128)S(1)} %collective-permute-done.1, ...), kind=kLoop, calls=%fused_computation.118 | loop fusion | flops 4464000 | bytes 9226944 | tf_op jit(solution)/shard_map/mul | solution.py:63
  124.3 5.6 %fusion.81 = (f32[62,40,90]{0,1,2:T(8,128)}, f32[62,40,90]{0,1,2:T(8,128)}, f32[62,40,90]{0,1,2:T(8,128)}, f32[62,40,90]{0,1,2:T(8,128)}) fusion(f32[126,40,2]{0,1,2:T(8,128)S(1)} %collective-permute-done.2, f32[1,40,90]{0,1,2:T(8,128)S(1)} %copy-done.6, f32[1,40,90]{0,1,2:T(8,128)S(1)} %copy-done.4, f32[124,40,90]{0,1,2:T(8,128)S(1)} %copy-done.8, ...), kind=kLoop, calls=%fused_computation.136 | loop fusion | flops 3571200 | bytes 9037440 | tf_op jit(solution)/shard_map/mul | solution.py:63
  129.9 15.1 %fusion.42 = f32[2,62,40,90]{1,2,3,0:T(8,128)} fusion(f32[2,62,42,92]{1,2,3,0:T(8,128)S(1)} %fusion.10, f32[2,62,40,90]{1,2,3,0:T(8,128)} %bitcast.51, f32[2,62,42,94]{1,2,3,0:T(8,128)} %get-tuple-element.51, f32[2,62,42,94]{1,2,3,0:T(8,128)} %get-tuple-element.50, f32[2,62,40,2]{1,2,3,0:T(8,128)S(1)} %collective-permute-done.5, ...), kind=kLoop, calls=%fused_computation.65 | loop fusion | flops 13392000 | bytes 23292160 | tf_op jit(solution)/shard_map/add | solution.py:78
  144.9 0.9 fusion.130
  145.9 4.7 %collective-permute-start.8 = (f32[2,62,40,2]{1,2,3,0:T(8,128)S(1)}, f32[2,62,40,2]{1,2,3,0:T(8,128)S(1)}, u32[]{:S(2)}, u32[]{:S(2)}) collective-permute-start(f32[2,62,40,2]{1,2,3,0:T(8,128)S(1)} %get-tuple-element.55), channel_id=1, source_target_pairs={{4,0},{8,4},{12,8},{16,12},{20,16},{24,20},{28,24},{0,28},{5,1},{9... | collective-permute-start | bytes 119048 | tf_op jit(solution)/shard_map/ppermute | solution.py:29
  150.7 2.5 copy.185
  153.2 1.7 pad_maximum_fusion.27
  155.6 3.6 collective-permute-done.10
  159.1 3.0 collective-permute-done.11
  162.1 1.0 pad_maximum_fusion.3
  163.1 4.2 %pad_maximum_fusion.2 = (f32[2,62,42,94]{1,2,3,0:T(8,128)}, f32[2,62,42,94]{1,2,3,0:T(8,128)}) fusion(f32[2,62,2,94]{1,2,3,0:T(2,128)S(1)} %collective-permute-done.10, f32[2,62,40,2]{1,2,3,0:T(8,128)S(1)} %collective-permute-done.8, f32[2,62,40,90]{1,2,3,0:T(8,128)S(1)} %copy-done.3, f32[2,62,40,2]{1,2,3,0:T(8,128)S(1)} %collective-permute-done.9, ...), kind=kLoop, calls=%fused_computation.3 | loop fusion | flops 2937312 | bytes 5967872 | tf_op jit(solution)/shard_map/concatenate | solution.py:25
  167.3 7.8 %fusion.2 = f32[2,62,42,92]{1,2,3,0:T(8,128)S(1)} fusion(f32[2,62,42,94]{1,2,3,0:T(8,128)} %get-tuple-element.47, f32[2,62,42,94]{1,2,3,0:T(8,128)} %get-tuple-element.46, f32[2,62,44,94]{1,2,3,0:T(8,128)S(1)} %pad_maximum_fusion.3, f32[62,42,92]{0,1,2:T(8,128)} %get-tuple-element.63, f32[62,42,92]{0,1,2:T(8,128)} %get-tuple-element.64, ...), kind=kLoop, calls=%fused_computation.9 | loop fusion | flops 5749632 | bytes 15347808 | tf_op jit(solution)/shard_map/mul | solution.py:75
  175.1 14.7 %fusion.20 = f32[2,62,40,90]{1,2,3,0:T(8,128)} fusion(f32[2,62,42,92]{1,2,3,0:T(8,128)S(1)} %fusion.2, f32[2,62,40,90]{1,2,3,0:T(8,128)} %fusion.42, f32[2,62,42,94]{1,2,3,0:T(8,128)} %get-tuple-element.47, f32[2,62,42,94]{1,2,3,0:T(8,128)} %get-tuple-element.46, f32[2,62,40,2]{1,2,3,0:T(8,128)S(1)} %collective-permute-done.9, ...), kind=kLoop, calls=%fused_computation.35 | loop fusion | flops 13392000 | bytes 23292160 | tf_op jit(solution)/shard_map/add | solution.py:78
  189.8 2.9 fusion.65
  192.8 4.7 %collective-permute-start.12 = (f32[40,1]{0,1:T(1,128)S(1)}, f32[40,1]{0,1:T(1,128)S(1)}, u32[]{:S(2)}, u32[]{:S(2)}) collective-permute-start(f32[40,1]{0,1:T(1,128)S(1)} %get-tuple-element.76), channel_id=1, source_target_pairs={{4,0},{8,4},{12,8},{16,12},{20,16},{24,20},{28,24},{0,28},{5,1},{9... | collective-permute-start | bytes 488 | tf_op jit(solution)/shard_map/ppermute | solution.py:29
  197.5 1.5 collective-permute-done.13
  199.7 1.5 collective-permute-done.14
  201.2 1.5 collective-permute-done.15
  203.5 39.8 %all-reduce.2 = (f32[]{:T(128)}, f32[]{:T(128)}) all-reduce(f32[]{:T(128)} %get-tuple-element.19, f32[]{:T(128)} %get-tuple-element.18), channel_id=1, replica_groups=mesh['gx'=8,'gy'=4] {'gx','gy'}, use_global_device_ids=true, to_apply=%region_2.3 | all-reduce | flops 2 | bytes 16 | tf_op jit(solution)/shard_map/psum | solution.py:162
  244.7 2.5 collective-permute-start.17
  247.2 2.3 collective-permute-start.16
  249.4 1.5 collective-permute-done.17
  251.8 1.1 collective-permute-done.18
  252.8 3.1 collective-permute-done.19
  256.7 40.3 %all-reduce.1 = (f32[]{:T(128)}, f32[]{:T(128)}) all-reduce(f32[]{:T(128)} %get-tuple-element.17, f32[]{:T(128)} %get-tuple-element.16), channel_id=1, replica_groups=mesh['gx'=8,'gy'=4] {'gx','gy'}, use_global_device_ids=true, to_apply=%region_6.7 | all-reduce | flops 2 | bytes 16 | tf_op jit(solution)/shard_map/psum | solution.py:162
  301.5 2.5 collective-permute-start.21
  304.0 2.2 collective-permute-start.20
  306.3 5.8 %copy.184 = f32[2,2,62,40,45]{4,3,0,2,1:T(8,128)} copy(f32[2,2,62,40,45]{2,3,4,0,1:T(8,128)} %bitcast.56) | data formatting | bytes 3571200 | tf_op jit(solution)/shard_map/reshape | solution.py:100
  312.1 6.4 %reshape.69 = f32[2,2,62,1800]{3,0,2,1:T(2,128)} reshape(f32[2,2,62,40,45]{4,3,0,2,1:T(8,128)} %copy.184) | data formatting | bytes 3571200 | tf_op jit(solution)/shard_map/reshape | solution.py:100
  319.1 6.4 %convolution_select_fusion = f32[2,2,62,1800]{3,0,2,1:T(2,128)S(1)} fusion(f32[2,2,62,1800]{3,0,2,1:T(2,128)} %reshape.69, pred[2]{0:T(512)(128)(4,1)S(1)} %broadcast_compare_fusion, f32[2,2,62,1800]{3,1,2,0:T(2,128)} %param.10, s32[2]{0:T(128)S(1)} %fusion.120), kind=kOutput, calls=%fused_computation.90 | convolution fusion | flops 11160004 | bytes 5356810 | tf_op jit(solution)/shard_map/ps,p...->s.../dot_general | solution.py:101
  325.5 2.2 copy.176
  328.6 38.3 %all-reduce = (f32[]{:T(128)}, f32[]{:T(128)}) all-reduce(f32[]{:T(128)} %get-tuple-element.15, f32[]{:T(128)} %get-tuple-element.14), channel_id=1, replica_groups=mesh['gx'=8,'gy'=4] {'gx','gy'}, use_global_device_ids=true, to_apply=%region_10.11 | all-reduce | flops 2 | bytes 16 | tf_op jit(solution)/shard_map/psum | solution.py:162
  (97 shorter events, 10.1 us)
Async XLA Ops:
  0.6 32.2 %copy-start = (f32[2,2,62,1800]{3,1,2,0:T(2,128)S(1)}, f32[2,2,62,1800]{3,1,2,0:T(2,128)}, u32[]{:S(2)}) copy-start(f32[2,2,62,1800]{3,1,2,0:T(2,128)} %param.9) | copy-start | bytes 5356804
  14.7 13.1 %copy-start.14 = (s32[2,1800]{1,0:T(2,128)S(1)}, s32[2,1800]{1,0:T(2,128)}, u32[]{:S(2)}) copy-start(s32[2,1800]{1,0:T(2,128)} %param.7) | copy-start | bytes 43204
  14.7 13.3 %copy-start.15 = (f32[2,1800]{1,0:T(2,128)S(1)}, f32[2,1800]{1,0:T(2,128)}, u32[]{:S(2)}) copy-start(f32[2,1800]{1,0:T(2,128)} %param.8) | copy-start | bytes 43204
  21.5 51.7 %collective-permute-start.5 = (f32[2,62,40,2]{1,2,3,0:T(8,128)S(1)}, f32[2,62,40,2]{1,2,3,0:T(8,128)S(1)}, u32[]{:S(2)}, u32[]{:S(2)}) collective-permute-start(f32[2,62,40,2]{1,2,3,0:T(8,128)S(1)} %get-tuple-element.56), channel_id=1, source_target_pairs={{0,4},{4,8},{8,12},{12,16},{16,20},{20,24},{24,28},{28,0},{1,5},{5... | collective-permute-start | bytes 119048 | tf_op jit(solution)/shard_map/ppermute | solution.py:27
  24.5 48.7 %collective-permute-start = (f32[2,62,40,2]{1,2,3,0:T(8,128)S(1)}, f32[2,62,40,2]{1,2,3,0:T(8,128)S(1)}, u32[]{:S(2)}, u32[]{:S(2)}) collective-permute-start(f32[2,62,40,2]{1,2,3,0:T(8,128)S(1)} %get-tuple-element.57), channel_id=1, source_target_pairs={{4,0},{8,4},{12,8},{16,12},{20,16},{24,20},{28,24},{0,28},{5,1},{9... | collective-permute-start | bytes 119048 | tf_op jit(solution)/shard_map/ppermute | solution.py:29
  53.1 5.0 %copy-start.4 = (f32[1,40,90]{0,1,2:T(8,128)S(1)}, f32[1,40,90]{0,1,2:T(8,128)}, u32[]{:S(2)}) copy-start(f32[1,40,90]{0,1,2:T(8,128)} %copy.162) | copy-start | bytes 43204
  58.1 5.9 %copy-start.9 = (f32[2,2,62,40,45]{4,3,2,1,0:T(8,128)S(1)}, f32[2,2,62,40,45]{4,3,2,1,0:T(8,128)}, u32[]{:S(2)}) copy-start(f32[2,2,62,40,45]{4,3,2,1,0:T(8,128)} %reshape.61) | copy-start | bytes 5356804
  59.2 16.3 %collective-permute-start.1 = (f32[126,40,2]{0,1,2:T(8,128)S(1)}, f32[126,40,2]{0,1,2:T(8,128)S(1)}, u32[]{:S(2)}, u32[]{:S(2)}) collective-permute-start(f32[126,40,2]{0,1,2:T(8,128)S(1)} %get-tuple-element.42), channel_id=1, source_target_pairs={{0,4},{4,8},{8,12},{12,16},{16,20},{20,24},{24,28},{28,0},{1,5},{5... | collective-permute-start | bytes 120968 | tf_op jit(solution)/shard_map/ppermute | solution.py:27
  59.3 16.2 %collective-permute-start.2 = (f32[126,40,2]{0,1,2:T(8,128)S(1)}, f32[126,40,2]{0,1,2:T(8,128)S(1)}, u32[]{:S(2)}, u32[]{:S(2)}) collective-permute-start(f32[126,40,2]{0,1,2:T(8,128)S(1)} %get-tuple-element.43), channel_id=1, source_target_pairs={{4,0},{8,4},{12,8},{16,12},{20,16},{24,20},{28,24},{0,28},{5,1},{9... | collective-permute-start | bytes 120968 | tf_op jit(solution)/shard_map/ppermute | solution.py:29
  73.2 2.3 copy-start.5
  73.2 2.5 copy-start.7
  74.9 7.2 %copy-start.2 = (f32[2,62,40,2,45]{1,2,4,3,0:T(8,128)S(1)}, f32[2,62,40,2,45]{1,2,4,3,0:T(8,128)}, u32[]{:S(2)}) copy-start(f32[2,62,40,2,45]{1,2,4,3,0:T(8,128)} %copy.155) | copy-start | bytes 5356804
  74.9 4.4 %collective-permute-start.6 = (f32[2,62,2,94]{1,2,3,0:T(2,128)S(1)}, f32[2,62,2,94]{1,2,3,0:T(2,128)S(1)}, u32[]{:S(2)}, u32[]{:S(2)}) collective-permute-start(f32[2,62,2,94]{1,2,3,0:T(2,128)S(1)} %get-tuple-element.52), channel_id=1, source_target_pairs={{1,0},{2,1},{3,2},{0,3},{5,4},{6,5},{7,6},{4,7},{9,8},{10,9},{11,1... | collective-permute-start | bytes 279752 | tf_op jit(solution)/shard_map/ppermute | solution.py:29
  75.1 7.1 %collective-permute-start.7 = (f32[2,62,2,94]{1,2,3,0:T(2,128)S(1)}, f32[2,62,2,94]{1,2,3,0:T(2,128)S(1)}, u32[]{:S(2)}, u32[]{:S(2)}) collective-permute-start(f32[2,62,2,94]{1,2,3,0:T(2,128)S(1)} %get-tuple-element.53), channel_id=1, source_target_pairs={{0,1},{1,2},{2,3},{3,0},{4,5},{5,6},{6,7},{7,4},{8,9},{9,10},{10,1... | collective-permute-start | bytes 279752 | tf_op jit(solution)/shard_map/ppermute | solution.py:27
  76.2 12.8 %collective-permute-start.3 = (f32[126,2,94]{0,1,2:T(2,128)S(1)}, f32[126,2,94]{0,1,2:T(2,128)S(1)}, u32[]{:S(2)}, u32[]{:S(2)}) collective-permute-start(f32[126,2,94]{0,1,2:T(2,128)S(1)} %get-tuple-element.40), channel_id=1, source_target_pairs={{0,1},{1,2},{2,3},{3,0},{4,5},{5,6},{6,7},{7,4},{8,9},{9,10},{10,1... | collective-permute-start | bytes 284264 | tf_op jit(solution)/shard_map/ppermute | solution.py:27
  77.3 11.8 %collective-permute-start.4 = (f32[126,2,94]{0,1,2:T(2,128)S(1)}, f32[126,2,94]{0,1,2:T(2,128)S(1)}, u32[]{:S(2)}, u32[]{:S(2)}) collective-permute-start(f32[126,2,94]{0,1,2:T(2,128)S(1)} %get-tuple-element.41), channel_id=1, source_target_pairs={{1,0},{2,1},{3,2},{0,3},{5,4},{6,5},{7,6},{4,7},{9,8},{10,9},{11,1... | collective-permute-start | bytes 284264 | tf_op jit(solution)/shard_map/ppermute | solution.py:29
  104.3 12.2 %copy-start.6 = (f32[1,40,90]{0,1,2:T(8,128)S(1)}, f32[1,40,90]{0,1,2:T(8,128)}, u32[]{:S(2)}) copy-start(f32[1,40,90]{0,1,2:T(8,128)} %copy.163) | copy-start | bytes 43204
  104.3 12.2 %copy-start.8 = (f32[124,40,90]{0,1,2:T(8,128)S(1)}, f32[124,40,90]{0,1,2:T(8,128)}, u32[]{:S(2)}) copy-start(f32[124,40,90]{0,1,2:T(8,128)} %reshape_reshape.3) | copy-start | bytes 5356804
  116.5 7.8 %copy-start.12 = (f32[1,62,40,2,45]{1,2,4,3,0:T(8,128)S(1)}, f32[1,62,40,2,45]{1,2,4,3,0:T(8,128)}, u32[]{:S(2)}) copy-start(f32[1,62,40,2,45]{1,2,4,3,0:T(8,128)} %copy.166) | copy-start | bytes 2678404
  145.9 7.3 %collective-permute-start.9 = (f32[2,62,40,2]{1,2,3,0:T(8,128)S(1)}, f32[2,62,40,2]{1,2,3,0:T(8,128)S(1)}, u32[]{:S(2)}, u32[]{:S(2)}) collective-permute-start(f32[2,62,40,2]{1,2,3,0:T(8,128)S(1)} %get-tuple-element.54), channel_id=1, source_target_pairs={{0,4},{4,8},{8,12},{12,16},{16,20},{20,24},{24,28},{28,0},{1,5},{5... | collective-permute-start | bytes 119048 | tf_op jit(solution)/shard_map/ppermute | solution.py:27
  145.9 7.3 %collective-permute-start.8 = (f32[2,62,40,2]{1,2,3,0:T(8,128)S(1)}, f32[2,62,40,2]{1,2,3,0:T(8,128)S(1)}, u32[]{:S(2)}, u32[]{:S(2)}) collective-permute-start(f32[2,62,40,2]{1,2,3,0:T(8,128)S(1)} %get-tuple-element.55), channel_id=1, source_target_pairs={{4,0},{8,4},{12,8},{16,12},{20,16},{24,20},{28,24},{0,28},{5,1},{9... | collective-permute-start | bytes 119048 | tf_op jit(solution)/shard_map/ppermute | solution.py:29
  153.2 8.9 %copy-start.3 = (f32[2,62,40,90]{1,2,3,0:T(8,128)S(1)}, f32[2,62,40,90]{1,2,3,0:T(8,128)}, u32[]{:S(2)}) copy-start(f32[2,62,40,90]{1,2,3,0:T(8,128)} %fusion.42) | copy-start | bytes 5356804
  154.9 4.2 %collective-permute-start.10 = (f32[2,62,2,94]{1,2,3,0:T(2,128)S(1)}, f32[2,62,2,94]{1,2,3,0:T(2,128)S(1)}, u32[]{:S(2)}, u32[]{:S(2)}) collective-permute-start(f32[2,62,2,94]{1,2,3,0:T(2,128)S(1)} %get-tuple-element.48), channel_id=1, source_target_pairs={{1,0},{2,1},{3,2},{0,3},{5,4},{6,5},{7,6},{4,7},{9,8},{10,9},{11,1... | collective-permute-start | bytes 279752 | tf_op jit(solution)/shard_map/ppermute | solution.py:29
  155.0 7.1 %collective-permute-start.11 = (f32[2,62,2,94]{1,2,3,0:T(2,128)S(1)}, f32[2,62,2,94]{1,2,3,0:T(2,128)S(1)}, u32[]{:S(2)}, u32[]{:S(2)}) collective-permute-start(f32[2,62,2,94]{1,2,3,0:T(2,128)S(1)} %get-tuple-element.49), channel_id=1, source_target_pairs={{0,1},{1,2},{2,3},{3,0},{4,5},{5,6},{6,7},{7,4},{8,9},{9,10},{10,1... | collective-permute-start | bytes 279752 | tf_op jit(solution)/shard_map/ppermute | solution.py:27
  163.1 4.2 %copy-start.10 = (f32[62,42,92]{0,1,2:T(8,128)S(1)}, f32[62,42,92]{0,1,2:T(8,128)}, u32[]{:S(2)}) copy-start(f32[62,42,92]{0,1,2:T(8,128)} %get-tuple-element.61) | copy-start | bytes 2874820
  167.3 7.8 %copy-start.11 = (f32[62,40,90]{0,1,2:T(8,128)S(1)}, f32[62,40,90]{0,1,2:T(8,128)}, u32[]{:S(2)}) copy-start(f32[62,40,90]{0,1,2:T(8,128)} %get-tuple-element.32) | copy-start | bytes 2678404
  189.8 9.8 %copy-start.13 = (f32[40,90]{1,0:T(8,128)S(1)}, f32[40,90]{1,0:T(8,128)}, u32[]{:S(2)}) copy-start(f32[40,90]{1,0:T(8,128)} %param.11) | copy-start | bytes 43204
  189.8 62.0 %copy-start.16 = (s32[2]{0:T(128)S(1)}, s32[2]{0:T(128)}, u32[]{:S(2)}) copy-start(s32[2]{0:T(128)} %param.6) | copy-start | bytes 28
  192.7 6.3 %collective-permute-start.13 = (f32[40,1]{0,1:T(1,128)S(1)}, f32[40,1]{0,1:T(1,128)S(1)}, u32[]{:S(2)}, u32[]{:S(2)}) collective-permute-start(f32[40,1]{0,1:T(1,128)S(1)} %get-tuple-element.75), channel_id=1, source_target_pairs={{0,4},{4,8},{8,12},{12,16},{16,20},{20,24},{24,28},{28,0},{1,5},{5... | collective-permute-start | bytes 488 | tf_op jit(solution)/shard_map/ppermute | solution.py:27
  192.8 6.3 %collective-permute-start.12 = (f32[40,1]{0,1:T(1,128)S(1)}, f32[40,1]{0,1:T(1,128)S(1)}, u32[]{:S(2)}, u32[]{:S(2)}) collective-permute-start(f32[40,1]{0,1:T(1,128)S(1)} %get-tuple-element.76), channel_id=1, source_target_pairs={{4,0},{8,4},{12,8},{16,12},{20,16},{24,20},{28,24},{0,28},{5,1},{9... | collective-permute-start | bytes 488 | tf_op jit(solution)/shard_map/ppermute | solution.py:29
  199.1 2.1 collective-permute-start.14
  199.1 3.6 collective-permute-start.15
  244.7 6.3 %collective-permute-start.17 = (f32[40,1]{0,1:T(1,128)S(1)}, f32[40,1]{0,1:T(1,128)S(1)}, u32[]{:S(2)}, u32[]{:S(2)}) collective-permute-start(f32[40,1]{0,1:T(1,128)S(1)} %get-tuple-element.71), channel_id=1, source_target_pairs={{0,4},{4,8},{8,12},{12,16},{16,20},{20,24},{24,28},{28,0},{1,5},{5... | collective-permute-start | bytes 488 | tf_op jit(solution)/shard_map/ppermute | solution.py:27
  247.2 3.8 %collective-permute-start.16 = (f32[40,1]{0,1:T(1,128)S(1)}, f32[40,1]{0,1:T(1,128)S(1)}, u32[]{:S(2)}, u32[]{:S(2)}) collective-permute-start(f32[40,1]{0,1:T(1,128)S(1)} %get-tuple-element.72), channel_id=1, source_target_pairs={{4,0},{8,4},{12,8},{16,12},{20,16},{24,20},{28,24},{0,28},{5,1},{9... | collective-permute-start | bytes 488 | tf_op jit(solution)/shard_map/ppermute | solution.py:29
  251.1 1.8 collective-permute-start.18
  251.1 4.8 %collective-permute-start.19 = (f32[1,92]{0,1:T(8,128)S(1)}, f32[1,92]{0,1:T(8,128)S(1)}, u32[]{:S(2)}, u32[]{:S(2)}) collective-permute-start(f32[1,92]{0,1:T(8,128)S(1)} %get-tuple-element.70), channel_id=1, source_target_pairs={{0,1},{1,2},{2,3},{3,0},{4,5},{5,6},{6,7},{7,4},{8,9},{9,10},{10,1... | collective-permute-start | bytes 1112 | tf_op jit(solution)/shard_map/ppermute | solution.py:27
  301.5 17.0 %collective-permute-start.21 = (f32[40,1]{0,1:T(1,128)S(1)}, f32[40,1]{0,1:T(1,128)S(1)}, u32[]{:S(2)}, u32[]{:S(2)}) collective-permute-start(f32[40,1]{0,1:T(1,128)S(1)} %get-tuple-element.67), channel_id=1, source_target_pairs={{0,4},{4,8},{8,12},{12,16},{16,20},{20,24},{24,28},{28,0},{1,5},{5... | collective-permute-start | bytes 488 | tf_op jit(solution)/shard_map/ppermute | solution.py:27
  304.0 14.5 %collective-permute-start.20 = (f32[40,1]{0,1:T(1,128)S(1)}, f32[40,1]{0,1:T(1,128)S(1)}, u32[]{:S(2)}, u32[]{:S(2)}) collective-permute-start(f32[40,1]{0,1:T(1,128)S(1)} %get-tuple-element.68), channel_id=1, source_target_pairs={{4,0},{8,4},{12,8},{16,12},{20,16},{24,20},{28,24},{0,28},{5,1},{9... | collective-permute-start | bytes 488 | tf_op jit(solution)/shard_map/ppermute | solution.py:29
  318.6 9.1 %collective-permute-start.22 = (f32[1,92]{0,1:T(8,128)S(1)}, f32[1,92]{0,1:T(8,128)S(1)}, u32[]{:S(2)}, u32[]{:S(2)}) collective-permute-start(f32[1,92]{0,1:T(8,128)S(1)} %get-tuple-element.65), channel_id=1, source_target_pairs={{1,0},{2,1},{3,2},{0,3},{5,4},{6,5},{7,6},{4,7},{9,8},{10,9},{11,1... | collective-permute-start | bytes 1112 | tf_op jit(solution)/shard_map/ppermute | solution.py:29
  318.6 9.1 %collective-permute-start.23 = (f32[1,92]{0,1:T(8,128)S(1)}, f32[1,92]{0,1:T(8,128)S(1)}, u32[]{:S(2)}, u32[]{:S(2)}) collective-permute-start(f32[1,92]{0,1:T(8,128)S(1)} %get-tuple-element.66), channel_id=1, source_target_pairs={{0,1},{1,2},{2,3},{3,0},{4,5},{5,6},{6,7},{7,4},{8,9},{9,10},{10,1... | collective-permute-start | bytes 1112 | tf_op jit(solution)/shard_map/ppermute | solution.py:27
  319.1 52.5 %copy-start.1 = (f32[2,2,62,1800]{3,1,2,0:T(2,128)S(1)}, f32[2,2,62,1800]{3,1,2,0:T(2,128)}, u32[]{:S(2)}) copy-start(f32[2,2,62,1800]{3,1,2,0:T(2,128)} %param.9) | copy-start | bytes 5356804
where the time goes:
time: 377 us; the launch traced here: 372 us
  blocking collectives  118 us (31%)
  other arithmetic  96.3 us (26%)
  local copies, waits for them, and re-layouts  71.5 us (19%)
  starting transfers between devices  35 us (9%)
  waiting for transfers between devices  20.7 us (5%)
  matrix products  18.8 us (5%)
  between operations  11 us (3%)
    psum x3, blocking collectives, two_products(): lax.psum((jnp.sum(residual * residual), jnp.sum(residual * applied)), ('g...  118 us
    add x2, other arithmetic, tracer_pass(): window(padded, 2, 0, 0)  29.8 us
    ppermute x12, starting transfers between devices, with_halo(): lax.ppermute(head, axis, [((i + 1) % count, i) for i in range(count)])  23 us
    mul x2, other arithmetic, tracer_pass(): scaled = window(mixing, 1, 0, 0) * first_lap  20 us
    transpose x2, local copies, waits for them, and re-layouts, to_strip(): return placed.transpose(axes_order).reshape(middle + (BY, slot_count * BX))  14.5 us
    ppermute x12, waiting for transfers between devices, with_halo(): lax.ppermute(tail, axis, [(i, (i + 1) % count) for i in range(count)])  13.5 us
    mul x2, other arithmetic, face_flux(): face_wet * face_speed * (0.5 * (centre + window(values, 2, step_y, step_x)))  13.4 us
    concatenate x8, other arithmetic, with_halo(): jnp.concatenate([lax.ppermute(tail, axis, [(i, (i + 1) % count) for i in...  13.3 us
  transfers between devices with their start and end apart: 24, of which 10 were waited for; matrix products, arithmetic and copies ran while one was open for 20% of the time, Pallas kernels for 0%

commit v1 on v0

v1 whole, which is shorter than its diff:
```python
import functools
import math

import jax
import jax.numpy as jnp
from jax import lax
from jax.experimental import pallas as pl
from jax.experimental.pallas import tpu as pltpu
from jax.sharding import PartitionSpec as P

BX = 45
BY = 40
PASSES = 2
ITERS = 3

advect_rate = 0.25
mixing_rate = 0.015
salt_weight = 0.8

HALO = 4
X0 = 16
C0 = 8
HALF = 64
MESH = pl.DeviceIdType.MESH
CENTRE = 4.25
SPREAD = 4.25


def kernel(
    gx_count, gy_count, bl_ref, wet_ref, mix_ref, vel_ref, tr_ref, damp_ref, out_ref, sh_ref,
    tmp, cells, strip, adv, w_, u_, n_, m_, we, wn, ce, cn, g_, colsend, colrecv, corner,
    frame, sideframe, vertframe, redx, redy,
    col_sem, row_sem, corner_sem, side_sem, vert_sem, redx_sem, redy_sem,
):
    slots = tr_ref.shape[0]
    levels = tr_ref.shape[2]
    water = tr_ref.shape[3]
    span = slots * BX
    rows = BY + 2 * HALO
    chunks = water // 128
    tail = water - 128 * chunks
    width_vregs = (span + 2 * 4 + 6) // 8
    gx = lax.axis_index("gx")
    gy = lax.axis_index("gy")
    east = lax.rem(gx + 1, gx_count)
    west = lax.rem(gx + gx_count - 1, gx_count)
    has_n = gy < gy_count - 1
    has_s = gy > 0

    for a in range(2):
        for y in list(range(HALO)) + list(range(rows - HALO, rows)):
            strip[a, y] = jnp.zeros(strip.shape[2:], jnp.float32)

    barrier = pltpu.get_barrier_semaphore()
    for k in range(1, gx_count):
        pl.semaphore_signal(barrier, inc=1, device_id=(lax.rem(gx + k, gx_count), gy), device_id_type=MESH)
    for k in range(1, gy_count):
        pl.semaphore_signal(barrier, inc=1, device_id=(gx, lax.rem(gy + k, gy_count)), device_id_type=MESH)

    for side in (west, east):
        for step in (1, gy_count - 1):
            other = lax.rem(gy + step, gy_count)
            pl.semaphore_signal(barrier, inc=1, device_id=(side, other), device_id_type=MESH)

    where_slot = []
    for s in range(slots):
        b = bl_ref[s]
        where_slot.append(jnp.where(b >= 0, lax.rem(b, slots), -1))

    for t in range(4):
        tmp[t] = jnp.zeros((128, 128), jnp.float32)

    def chosen(p, pieces):
        value = jnp.zeros_like(pieces[0])
        for s in range(slots):
            value = jnp.where(where_slot[s] == p, pieces[s], value)
        return value

    def bring(cols, lanes):
        for p in range(slots):
            for a, ref in enumerate((vel_ref, tr_ref)):
                t = 2 * a + p
                for n in range(2):
                    tmp[t, HALF * n : HALF * n + levels, 0:lanes] = chosen(
                        p, [ref[s, n, :, cols] for s in range(slots)]
                    )
            tmp[p, levels : levels + 1, 0:lanes] = chosen(
                p, [wet_ref[s : s + 1, cols].astype(jnp.float32) for s in range(slots)]
            )
            tmp[p, HALF + levels : HALF + levels + 1, 0:lanes] = chosen(
                p, [mix_ref[s : s + 1, cols] for s in range(slots)]
            )

    def bring_chunk(j, carry):
        base = pl.multiple_of(j * 128, 128)
        bring(pl.ds(base, 128), 128)
        for t in range(4):
            cells[t, pl.ds(base, 128), :] = tmp[t].T
        return carry

    lax.fori_loop(0, chunks, bring_chunk, 0)
    bring(pl.ds(chunks * 128, tail), tail)
    for t in range(4):
        cells[t, chunks * 128 : chunks * 128 + 128, :] = tmp[t].T

    for a in range(2):
        for p in range(slots):
            for y in range(BY):
                strip[a, HALO + y, X0 + BX * p : X0 + BX * (p + 1), :] = cells[
                    2 * a + p, BX * y : BX * (y + 1), :
                ]

    for a in range(2):
        for y in range(BY):
            colsend[0, a, y] = strip[a, HALO + y, X0 : X0 + HALO, :]
            colsend[1, a, y] = strip[a, HALO + y, X0 + span - HALO : X0 + span, :]

    pl.semaphore_wait(barrier, gx_count - 1 + gy_count - 1 + 4)

    def remote(src, dst, sems, index, device):
        return pltpu.make_async_remote_copy(
            src_ref=src, dst_ref=dst, send_sem=sems.at[0, index], recv_sem=sems.at[1, index],
            device_id=device, device_id_type=MESH,
        )

    to_west = remote(colsend.at[0], colrecv.at[1], col_sem, 1, (west, gy))
    to_east = remote(colsend.at[1], colrecv.at[0], col_sem, 0, (east, gy))
    to_west.start()
    to_east.start()
    inner = pl.ds(X0, 96)
    to_north = remote(
        strip.at[:, pl.ds(BY, HALO), inner], strip.at[:, pl.ds(0, HALO), inner], row_sem, 0, (gx, gy + 1)
    )
    to_south = remote(
        strip.at[:, pl.ds(HALO, HALO), inner], strip.at[:, pl.ds(BY + HALO, HALO), inner], row_sem, 1, (gx, gy - 1)
    )

    @pl.when(has_n)
    def _():
        to_north.start()

    @pl.when(has_s)
    def _():
        to_south.start()

    to_west.wait()
    to_east.wait()

    def corner_copy(vert, side):
        source = colrecv.at[side, :, pl.ds(BY - HALO if vert == 0 else 0, HALO)]
        device = (gx, gy + 1) if vert == 0 else (gx, gy - 1)
        return remote(source, corner.at[vert, side], corner_sem, 2 * vert + side, device)

    @pl.when(has_n)
    def _():
        for side in range(2):
            corner_copy(0, side).start()

    @pl.when(has_s)
    def _():
        for side in range(2):
            corner_copy(1, side).start()

    @pl.when(has_n)
    def _():
        to_north.wait_send()
        for side in range(2):
            corner_copy(0, side).wait_send()

    @pl.when(has_s)
    def _():
        to_south.wait_send()
        for side in range(2):
            corner_copy(1, side).wait_send()

    @pl.when(has_s)
    def _():
        to_north.wait_recv()
        for side in range(2):
            corner_copy(0, side).wait_recv()

    @pl.when(has_n)
    def _():
        to_south.wait_recv()
        for side in range(2):
            corner_copy(1, side).wait_recv()

    halo_columns = ((X0 - HALO, X0), (X0 + span, X0 + span + HALO))
    for a in range(2):
        for side, (lo, hi) in enumerate(halo_columns):
            for y in range(BY):
                strip[a, HALO + y, lo:hi, :] = colrecv[side, a, y]

    def put_corners(vert):
        base = 0 if vert == 0 else HALO + BY
        for a in range(2):
            for side, (lo, hi) in enumerate(halo_columns):
                for y in range(HALO):
                    strip[a, base + y, lo:hi, :] = corner[vert, side, a, y]

    @pl.when(has_s)
    def _():
        put_corners(0)

    @pl.when(has_n)
    def _():
        put_corners(1)

    lane = lax.broadcasted_iota(jnp.int32, (8, 128), 1)
    low = lane < HALF
    level = jnp.where(low, lane, lane - HALF).astype(jnp.float32)

    def prepare(y, depths):
        kept = []
        for v in range(width_vregs):
            here = pl.ds(C0 + 8 * v, 8)
            flow = strip[0, y, here, :]
            depth = jnp.broadcast_to(flow[:, levels : levels + 1], (8, 128))
            mixing = jnp.broadcast_to(flow[:, HALF + levels : HALF + levels + 1], (8, 128))
            turned = pltpu.roll(flow, HALF, 1)
            w_[y, here, :] = jnp.where(level < depth, 1.0, 0.0)
            u_[y, here, :] = jnp.where(low, flow, turned)
            n_[y, here, :] = jnp.where(low, turned, flow)
            m_[y, here, :] = mixing_rate * mixing
            kept.append(jnp.where(lane == y, depth, depths[v]))
        return tuple(kept)

    blank = tuple(jnp.zeros((8, 128), jnp.float32) for _ in range(width_vregs))
    depth_columns = lax.fori_loop(0, rows, prepare, blank)

    def faces(y, carry):
        for v in range(width_vregs):
            x = C0 + 8 * v
            here = pl.ds(x, 8)
            there = pl.ds(x + 1, 8)
            wet = w_[y, here, :]
            wet_e = wet * w_[y, there, :]
            wet_n = wet * w_[y + 1, here, :]
            we[y, here, :] = wet_e
            wn[y, here, :] = wet_n
            scale = advect_rate * 0.25
            ce[y, here, :] = (scale * wet_e) * (u_[y, here, :] + u_[y, there, :])
            cn[y, here, :] = (scale * wet_n) * (n_[y, here, :] + n_[y + 1, here, :])
        return carry

    lax.fori_loop(0, rows - 1, faces, 0)

    def first(f, y, carry):
        for v in range(width_vregs):
            x = C0 + 8 * v
            here, right, left = pl.ds(x, 8), pl.ds(x + 1, 8), pl.ds(x - 1, 8)
            mid = f[y, here, :]
            lap = (
                we[y, here, :] * (f[y, right, :] - mid)
                + we[y, left, :] * (f[y, left, :] - mid)
                + wn[y, here, :] * (f[y + 1, here, :] - mid)
                + wn[y - 1, here, :] * (f[y - 1, here, :] - mid)
            )
            g_[y, here, :] = m_[y, here, :] * lap
        return carry

    def second(f, y, v):
        x = C0 + 8 * v
        here, right, left = pl.ds(x, 8), pl.ds(x + 1, 8), pl.ds(x - 1, 8)
        mid = f[y, here, :]
        gm = g_[y, here, :]
        flow = (
            ce[y, here, :] * (mid + f[y, right, :])
            - ce[y, left, :] * (mid + f[y, left, :])
            + cn[y, here, :] * (mid + f[y + 1, here, :])
            - cn[y - 1, here, :] * (mid + f[y - 1, here, :])
        )
        mix = (
            we[y, here, :] * (g_[y, right, :] - gm)
            + we[y, left, :] * (g_[y, left, :] - gm)
            + wn[y, here, :] * (g_[y + 1, here, :] - gm)
            + wn[y - 1, here, :] * (g_[y - 1, here, :] - gm)
        )
        return mid - (flow + mix)

    old, new = strip.at[1], adv
    lax.fori_loop(1, rows - 1, functools.partial(first, old), 0)

    def pass_one(y, carry):
        for v in range(width_vregs):
            adv[y, pl.ds(C0 + 8 * v, 8), :] = second(old, y, v)
        return carry

    lax.fori_loop(2, rows - 2, pass_one, 0)
    lax.fori_loop(3, rows - 3, functools.partial(first, new), 0)
    weight = jnp.where(low, 1.0, -salt_weight) * (1.0 / math.sqrt(levels))

    def pass_two(y, sums):
        kept = []
        for v in range(width_vregs):
            here = pl.ds(C0 + 8 * v, 8)
            value = second(new, y, v)
            strip[1, y, here, :] = value
            total = jnp.sum(w_[y, here, :] * weight * value, axis=1, keepdims=True)
            kept.append(jnp.where(lane == y, jnp.broadcast_to(total, (8, 128)), sums[v]))
        return tuple(kept)

    forcing_columns = lax.fori_loop(HALO, HALO + BY, pass_two, blank)

    def to_grid(columns, t):
        for v in range(width_vregs):
            tmp[t, 8 * v : 8 * v + 8, :] = columns[v]
        if width_vregs < 16:
            tmp[t, 8 * width_vregs : 128, :] = jnp.zeros((128 - 8 * width_vregs, 128), jnp.float32)
        return tmp[t].T[0:rows, :]

    frame[0] = to_grid(forcing_columns, 0)
    depth_grid = to_grid(depth_columns, 1)
    shift = X0 - C0
    tmp[2, HALO : HALO + BY, 0:span] = damp_ref[...]
    frame[1] = pltpu.roll(tmp[2, 0:rows, :], shift, 1)

    def side_copy(side):
        device = (east, gy) if side == 0 else (west, gy)
        return remote(frame, sideframe.at[side], side_sem, side, device)

    def vert_copy(vert, column):
        target = (east, gx, west)[column]
        source = frame.at[:, pl.ds(rows - 8 if vert == 0 else 0, 8)]
        device = (target, gy + 1) if vert == 0 else (target, gy - 1)
        return remote(source, vertframe.at[vert, column], vert_sem, 3 * vert + column, device)

    for side in range(2):
        side_copy(side).start()

    @pl.when(has_n)
    def _():
        for column in range(3):
            vert_copy(0, column).start()

    @pl.when(has_s)
    def _():
        for column in range(3):
            vert_copy(1, column).start()

    for p in range(slots):
        for y in range(BY):
            cells[p, BX * y : BX * (y + 1), :] = strip[1, HALO + y, X0 + BX * p : X0 + BX * (p + 1), :]

    def give(cols, lanes, base):
        turned = [cells[p, pl.ds(base, 128), :].T for p in range(slots)]
        for s in range(slots):
            for n in range(2):
                value = tr_ref[s, n, :, cols]
                for p in range(slots):
                    piece = turned[p][HALF * n : HALF * n + levels, 0:lanes]
                    value = jnp.where(where_slot[s] == p, piece, value)
                out_ref[s, n, :, cols] = value

    def give_chunk(j, carry):
        base = pl.multiple_of(j * 128, 128)
        give(pl.ds(base, 128), 128, base)
        return carry

    lax.fori_loop(0, chunks, give_chunk, 0)
    give(pl.ds(chunks * 128, tail), tail, chunks * 128)

    for side in range(2):
        side_copy(side).wait()

    @pl.when(has_n)
    def _():
        for column in range(3):
            vert_copy(0, column).wait_send()

    @pl.when(has_s)
    def _():
        for column in range(3):
            vert_copy(1, column).wait_send()

    @pl.when(has_s)
    def _():
        for column in range(3):
            vert_copy(0, column).wait_recv()

    @pl.when(has_n)
    def _():
        for column in range(3):
            vert_copy(1, column).wait_recv()

    lanes = lax.broadcasted_iota(jnp.int32, (rows, 128), 1)
    ys = lax.broadcasted_iota(jnp.int32, (rows, 128), 0)
    sub = lax.broadcasted_iota(jnp.int32, (8, 128), 0)

    def extended(kind):
        parts = []
        for column, middle in enumerate((sideframe.at[0, kind], frame.at[kind], sideframe.at[1, kind])):
            south = jnp.where(has_s, vertframe[0, column, kind], 0.0)
            north = jnp.where(has_n, vertframe[1, column, kind], 0.0)
            first_rows = jnp.where(sub < HALO, south, middle[0:8, :])
            last_rows = jnp.where(sub < HALO, middle[rows - 8 : rows, :], north)
            parts.append(jnp.concatenate([first_rows, middle[8 : rows - 8, :], last_rows], axis=0))
        return jnp.where(
            lanes < shift,
            pltpu.roll(parts[0], 128 - span, 1),
            jnp.where(lanes < shift + span, parts[1], pltpu.roll(parts[2], span, 1)),
        )

    forcing = extended(0)
    damping = extended(1)

    def nbr_e(v):
        return pltpu.roll(v, 127, 1)

    def nbr_w(v):
        return pltpu.roll(v, 1, 1)

    def nbr_n(v):
        return pltpu.roll(v, rows - 1, 0)

    def nbr_s(v):
        return pltpu.roll(v, 1, 0)

    hops = (nbr_e, nbr_w, nbr_n, nbr_s)
    couplings = [jnp.minimum(depth_grid, hop(depth_grid)) / levels for hop in hops]
    diagonal = damping + (couplings[0] + couplings[1] + couplings[2] + couplings[3]) - CENTRE

    def shifted(v):
        beside = [c * hop(v) for c, hop in zip(couplings, hops)]
        return (diagonal * v - (beside[0] + beside[1] + beside[2] + beside[3])) * (1.0 / SPREAD)

    basis = [forcing, shifted(forcing)]
    while len(basis) < ITERS + 1:
        basis.append(2.0 * shifted(basis[-1]) - basis[-2])
    inside = (ys >= HALO) & (ys < HALO + BY) & (lanes >= shift) & (lanes < shift + span)
    pairs = ((0, 0), (0, 1), (1, 1), (1, 2), (2, 2), (2, 3), (0, 2), (0, 3))
    for k, (i, j) in enumerate(pairs):
        product = jnp.where(inside, basis[i] * basis[j], 0.0)
        redx[0, k : k + 1, :] = jnp.sum(product, axis=0, keepdims=True)

    def redx_copy(k):
        return remote(redx.at[0], redx.at[k], redx_sem, k, (lax.rem(gx + k, gx_count), gy))

    def redy_copy(k):
        return remote(redy.at[0], redy.at[k], redy_sem, k, (gx, lax.rem(gy + k, gy_count)))

    for k in range(1, gx_count):
        redx_copy(k).start()
    for k in range(1, gx_count):
        redx_copy(k).wait()
    total = redx[0]
    for k in range(1, gx_count):
        total = total + redx[k]
    redy[0] = total
    for k in range(1, gy_count):
        redy_copy(k).start()
    for k in range(1, gy_count):
        redy_copy(k).wait()
    total = redy[0]
    for k in range(1, gy_count):
        total = total + redy[k]
    total = jnp.broadcast_to(jnp.sum(total, axis=1, keepdims=True), (8, 128))
    gram = {}
    for k, (i, j) in enumerate(pairs):
        gram[i, j] = gram[j, i] = total[k : k + 1, :]
    gram[1, 3] = gram[3, 1] = gram[2, 2] + gram[1, 1] - gram[0, 0]

    def inner_product(a, b):
        value = None
        for i, ai in enumerate(a):
            for j, bj in enumerate(b):
                if ai is not None and bj is not None:
                    term = ai * bj * gram[i, j]
                    value = term if value is None else value + term
        return value

    def add(a, b):
        return b if a is None else a if b is None else a + b

    def combine(a, scale, b):
        return [add(ai, None if bi is None else scale * bi) for ai, bi in zip(a, b)]

    def image_of(p):
        image = [None] * (ITERS + 1)
        for i in range(ITERS):
            if p[i] is None:
                continue
            image[i] = add(image[i], CENTRE * p[i])
            if i == 0:
                image[1] = add(image[1], SPREAD * p[i])
            else:
                image[i + 1] = add(image[i + 1], (0.5 * SPREAD) * p[i])
                image[i - 1] = add(image[i - 1], (0.5 * SPREAD) * p[i])
        return image

    one = jnp.ones((1, 128), jnp.float32)
    residual = [one] + [None] * ITERS
    direction = [one] + [None] * ITERS
    height = [None] * (ITERS + 1)
    norm = gram[0, 0]
    for iteration in range(ITERS):
        image = image_of(direction)
        step = norm / inner_product(direction, image)
        height = combine(height, step, direction)
        if iteration + 1 < ITERS:
            residual = combine(residual, -step, image)
            norm_next = inner_product(residual, residual)
            direction = combine(residual, norm_next / norm, direction)
            norm = norm_next
    answer = height[0] * basis[0] + height[1] * basis[1] + height[2] * basis[2]
    answer = pltpu.roll(pltpu.roll(answer, 128 - shift, 1), rows - HALO, 0)
    sh_ref[...] = answer[0:BY, 0:span]


def per_device(block_list, wet_levels, mixing, velocity, tracers, damping):
    gx_count = lax.axis_size("gx")
    gy_count = lax.axis_size("gy")
    slots = tracers.shape[0]
    span = slots * BX
    rows = BY + 2 * HALO
    wide = -(-(X0 + span + HALO + 8) // 8) * 8
    f32 = jnp.float32
    big = pltpu.VMEM((rows, wide, 128), f32)
    vmem = pl.BlockSpec(memory_space=pltpu.VMEM)
    dma = pltpu.SemaphoreType.DMA
    cell_rows = -(-tracers.shape[3] // 128) * 128
    return pl.pallas_call(
        functools.partial(kernel, gx_count, gy_count),
        out_shape=(
            jax.ShapeDtypeStruct(tracers.shape, f32),
            jax.ShapeDtypeStruct(damping.shape, f32),
        ),
        in_specs=[pl.BlockSpec(memory_space=pltpu.SMEM)] + [vmem] * 5,
        out_specs=(vmem, vmem),
        scratch_shapes=[
            pltpu.VMEM((4, 128, 128), f32),
            pltpu.VMEM((4, cell_rows, 128), f32),
            pltpu.VMEM((2, rows, wide, 128), f32),
            big, big, big, big, big, big, big, big, big, big,
            pltpu.VMEM((2, 2, BY, HALO, 128), f32),
            pltpu.VMEM((2, 2, BY, HALO, 128), f32),
            pltpu.VMEM((2, 2, 2, HALO, HALO, 128), f32),
            pltpu.VMEM((2, rows, 128), f32),
            pltpu.VMEM((2, 2, rows, 128), f32),
            pltpu.VMEM((2, 3, 2, 8, 128), f32),
            pltpu.VMEM((gx_count, 8, 128), f32),
            pltpu.VMEM((gy_count, 8, 128), f32),
            dma((2, 2)), dma((2, 2)), dma((2, 4)), dma((2, 2)), dma((2, 6)),
            dma((2, gx_count)), dma((2, gy_count)),
        ],
        compiler_params=pltpu.CompilerParams(
            collective_id=0, has_side_effects=True, vmem_limit_bytes=62 * 1024 * 1024
        ),
        name="ocean",
    )(block_list, wet_levels, mixing, velocity, tracers, damping)


def solution(mesh):
    return jax.shard_map(
        per_device,
        mesh=mesh,
        in_specs=(
            P(("gx", "gy")),
            P(("gx", "gy"), None),
            P(("gx", "gy"), None),
            P(("gx", "gy"), None, None, None),
            P(("gx", "gy"), None, None, None),
            P("gy", "gx"),
        ),
        out_specs=(P(("gx", "gy"), None, None, None), P("gy", "gx")),
        check_vma=False,
    )
```

time: 377 us -> 61.6 us (0.16); the launches traced: 372 us -> 61.5 us
  blocking collectives: 118 us -> 0 us
  other arithmetic: 96.3 us -> 0 us
  local copies, waits for them, and re-layouts: 71.5 us -> 9.4 us
  Pallas kernels: 0 us -> 51.4 us
  starting transfers between devices: 35 us -> 0 us
  waiting for transfers between devices: 20.7 us -> 0 us
  matrix products: 18.8 us -> 0 us
  between operations: 11 us -> 0.66 us
    psum x3 -> x0, blocking collectives: 118 us -> none  [two_products(): lax.psum((jnp.sum(residual * residual), jnp.sum(residual * applied)), ('g...]
    pallas_call x0 -> x1, Pallas kernels: none -> 51.4 us  [per_device(): pl.pallas_call(functools.partial(kernel, gx_count, gy_count), out_shape=(...]
    mul x5 -> x0, other arithmetic: 37.2 us -> none  [the longest x2 20 us: tracer_pass(): scaled = window(mixing, 1, 0, 0) * first_lap]
    ppermute x24 -> x0, starting transfers between devices: 35 us -> none  [the longest x12 23 us: with_halo(): lax.ppermute(head, axis, [((i + 1) % count, i) for i in range(count)])]
    add x3 -> x0, other arithmetic: 29.8 us -> none  [the longest x2 29.8 us: tracer_pass(): window(padded, 2, 0, 0)]
    reshape x8 -> x0, local copies, waits for them, and re-layouts: 22.6 us -> none  [the longest x2 12.2 us: from_strip(): blocks.transpose(axes_order).reshape((slot_count,) + middle + (BY * BX,))]
    ppermute x24 -> x0, waiting for transfers between devices: 20.7 us -> none  [the longest x12 13.5 us: with_halo(): lax.ppermute(tail, axis, [(i, (i + 1) % count) for i in range(count)])]
    dot_general x5 -> x0, matrix products: 18.8 us -> none  [the longest x4 12.4 us: to_strip(): jnp.einsum('ps,s...->p...', selector, slot_values, precision=lax.Precisio...]
  transfers between devices with their start and end apart: 24 -> 0, of which waited for: 10 -> 0; matrix products, arithmetic and copies ran while one was open for 20% -> 0% of each run, Pallas kernels for 0% -> 0%
where the time goes in v1:
time: 61.6 us; the launch traced here: 61.5 us
  Pallas kernels  51.4 us (83%)
  local copies, waits for them, and re-layouts  9.4 us (15%)
  between operations  0.66 us (1%)
    pallas_call x1, Pallas kernels, per_device(): pl.pallas_call(functools.partial(kernel, gx_count, gy_count), out_shape=(...  51.4 us
    unnamed x7, local copies, waits for them, and re-layouts  5.13 us
    pallas_call x1, local copies, waits for them, and re-layouts, per_device(): pl.pallas_call(functools.partial(kernel, gx_count, gy_count), out_shape=(...  4.27 us

profile of v1, /device:TPU:0, one launch (start us, length us, event | category | flops | bytes accessed | tf_op | source)
XLA Modules:
  0.0 61.5 jit_solution(7067852343384983757)
XLA Ops:
  0.6 0.0 copy-start
  0.6 3.1 %copy.8.vel_ref = f32[2,2,62,1800]{3,2,1,0:T(8,128)} copy(f32[2,2,62,1800]{3,1,2,0:T(2,128)} %param.9) | data formatting | bytes 3571200 | tf_op args[3]
  3.7 0.0 copy-done
  3.7 1.4 %copy.9.tr_ref = f32[2,2,62,1800]{3,2,1,0:T(8,128)} copy(f32[2,2,62,1800]{3,1,2,0:T(2,128)S(1)} %copy-done) | data formatting | bytes 3571200 | tf_op args[4]
  5.2 51.4 %ocean.1 = (f32[2,2,62,1800]{3,2,1,0:T(8,128)}, f32[40,90]{1,0:T(8,128)}) custom-call(s32[2]{0:T(128)} %bl_ref.1, s32[2,1800]{1,0:T(2,128)} %wet_ref.1, f32[2,1800]{1,0:T(2,128)} %mix_ref.1, f32[2,2,62,1800]{3,2,1,0:T(8,128)} %copy.8.vel_ref, f32[2,2,62,1800]{3,2,1,0:T(8,128)} %copy.9.tr_ref, f32[40,90]{1,0:T(8,128)} %damp_ref.1), custom_call_target="tpu_custom_call" | custom-call | tf_op jit(solution)/shard_map/ocean/pallas_call | solution.py:522
  56.6 0.0 copy-start.1
  56.6 4.3 %copy.10 = f32[2,2,62,1800]{3,1,2,0:T(2,128)} copy(f32[2,2,62,1800]{3,2,1,0:T(8,128)} %get-tuple-element.2) | data formatting | bytes 3571200 | tf_op jit(solution)/shard_map/ocean/pallas_call | solution.py:522
  60.8 0.0 copy-done.1
  60.8 0.6 copy.12
Async XLA Ops:
  0.6 3.1 %copy-start = (f32[2,2,62,1800]{3,1,2,0:T(2,128)S(1)}, f32[2,2,62,1800]{3,1,2,0:T(2,128)}, u32[]{:S(2)}) copy-start(f32[2,2,62,1800]{3,1,2,0:T(2,128)} %param.10) | copy-start | bytes 5356804
  56.6 4.3 %copy-start.1 = (f32[40,90]{1,0:T(8,128)S(1)}, f32[40,90]{1,0:T(8,128)}, u32[]{:S(2)}) copy-start(f32[40,90]{1,0:T(8,128)} %get-tuple-element.7) | copy-start | bytes 43204

commit v2 on v1

v2 whole, which is shorter than its diff:
```python
import functools
import math

import jax
import jax.numpy as jnp
from jax import lax
from jax.experimental import pallas as pl
from jax.experimental.pallas import tpu as pltpu
from jax.sharding import PartitionSpec as P

BX = 45
BY = 40
PASSES = 2
ITERS = 3

advect_rate = 0.25
mixing_rate = 0.015
salt_weight = 0.8

HALO = 4
X0 = 16
C0 = 8
HALF = 64
MESH = pl.DeviceIdType.MESH


def kernel(
    gx_count, gy_count, bl_ref, wet_ref, mix_ref, vel_ref, tr_ref, damp_ref, out_ref, sh_ref,
    tmp, cells, strip, adv, w_, u_, n_, m_, we, wn, ce, cn, g_, colsend, colrecv, corner,
    frame, sideframe, vertframe, redx, redy, fitx, fity, out_v,
    col_sem, row_sem, corner_sem, side_sem, vert_sem, redx_sem, redy_sem, fitx_sem, fity_sem, out_sem,
):
    slots = tr_ref.shape[0]
    levels = tr_ref.shape[2]
    water = tr_ref.shape[3]
    span = slots * BX
    rows = BY + 2 * HALO
    chunks = water // 128
    tail = water - 128 * chunks
    width_vregs = (span + 2 * 4 + 6) // 8
    gx = lax.axis_index("gx")
    gy = lax.axis_index("gy")
    east = lax.rem(gx + 1, gx_count)
    west = lax.rem(gx + gx_count - 1, gx_count)
    has_n = gy < gy_count - 1
    has_s = gy > 0

    for a in range(2):
        for y in list(range(HALO)) + list(range(rows - HALO, rows)):
            strip[a, y] = jnp.zeros(strip.shape[2:], jnp.float32)

    barrier = pltpu.get_barrier_semaphore()
    for k in range(1, gx_count):
        pl.semaphore_signal(barrier, inc=1, device_id=(lax.rem(gx + k, gx_count), gy), device_id_type=MESH)
    for k in range(1, gy_count):
        pl.semaphore_signal(barrier, inc=1, device_id=(gx, lax.rem(gy + k, gy_count)), device_id_type=MESH)

    for side in (west, east):
        for step in (1, gy_count - 1):
            other = lax.rem(gy + step, gy_count)
            pl.semaphore_signal(barrier, inc=1, device_id=(side, other), device_id_type=MESH)

    where_slot = []
    for s in range(slots):
        b = bl_ref[s]
        where_slot.append(jnp.where(b >= 0, lax.rem(b, slots), -1))

    for t in range(4):
        tmp[t] = jnp.zeros((128, 128), jnp.float32)

    def chosen(p, pieces):
        value = jnp.zeros_like(pieces[0])
        for s in range(slots):
            value = jnp.where(where_slot[s] == p, pieces[s], value)
        return value

    def remote(src, dst, sems, index, device):
        return pltpu.make_async_remote_copy(
            src_ref=src, dst_ref=dst, send_sem=sems.at[0, index], recv_sem=sems.at[1, index],
            device_id=device, device_id_type=MESH,
        )

    def bring(a, ref, cols, lanes):
        for p in range(slots):
            t = 2 * a + p
            for n in range(2):
                tmp[t, HALF * n : HALF * n + levels, 0:lanes] = chosen(
                    p, [ref[s, n, :, cols] for s in range(slots)]
                )
            if a == 0:
                tmp[p, levels : levels + 1, 0:lanes] = chosen(
                    p, [wet_ref[s : s + 1, cols].astype(jnp.float32) for s in range(slots)]
                )
                tmp[p, HALF + levels : HALF + levels + 1, 0:lanes] = chosen(
                    p, [mix_ref[s : s + 1, cols] for s in range(slots)]
                )

    def col_copy(a, side):
        device = (east, gy) if side == 0 else (west, gy)
        return remote(colsend.at[side, a], colrecv.at[side, a], col_sem, 2 * a + side, device)

    inner = pl.ds(X0, 96)

    def row_copy(a, vert):
        source = strip.at[a, pl.ds(BY if vert == 0 else HALO, HALO), inner]
        target = strip.at[a, pl.ds(0 if vert == 0 else BY + HALO, HALO), inner]
        return remote(source, target, row_sem, 2 * a + vert, (gx, gy + 1) if vert == 0 else (gx, gy - 1))

    def corner_copy(vert, side):
        source = colrecv.at[side, :, pl.ds(BY - HALO if vert == 0 else 0, HALO)]
        device = (gx, gy + 1) if vert == 0 else (gx, gy - 1)
        return remote(source, corner.at[vert, side], corner_sem, 2 * vert + side, device)

    def side_copy(kind, side):
        device = (east, gy) if side == 0 else (west, gy)
        return remote(frame.at[kind], sideframe.at[side, kind], side_sem, 2 * kind + side, device)

    def vert_copy(kind, vert, column):
        target = (east, gx, west)[column]
        source = frame.at[kind, pl.ds(rows - 8 if vert == 0 else 0, 8)]
        device = (target, gy + 1) if vert == 0 else (target, gy - 1)
        index = 6 * kind + 3 * vert + column
        return remote(source, vertframe.at[vert, column, kind], vert_sem, index, device)

    senders = (has_n, has_s)
    receivers = (has_s, has_n)

    for a, ref in enumerate((vel_ref, tr_ref)):

        def bring_chunk(j, carry):
            base = pl.multiple_of(j * 128, 128)
            bring(a, ref, pl.ds(base, 128), 128)
            for t in range(2 * a, 2 * a + 2):
                cells[t, pl.ds(base, 128), :] = tmp[t].T
            return carry

        lax.fori_loop(0, chunks, bring_chunk, 0)
        bring(a, ref, pl.ds(chunks * 128, tail), tail)
        for t in range(2 * a, 2 * a + 2):
            cells[t, chunks * 128 : chunks * 128 + 128, :] = tmp[t].T
        for p in range(slots):
            for y in range(BY):
                strip[a, HALO + y, X0 + BX * p : X0 + BX * (p + 1), :] = cells[
                    2 * a + p, BX * y : BX * (y + 1), :
                ]
        for y in range(BY):
            colsend[0, a, y] = strip[a, HALO + y, X0 + span - HALO : X0 + span, :]
            colsend[1, a, y] = strip[a, HALO + y, X0 : X0 + HALO, :]
        if a == 0:
            pl.semaphore_wait(barrier, gx_count - 1 + gy_count - 1 + 4)
        for side in range(2):
            col_copy(a, side).start()
        for vert in range(2):

            @pl.when(senders[vert])
            def _():
                row_copy(a, vert).start()

    shift = X0 - C0
    tmp[2, HALO : HALO + BY, 0:span] = damp_ref[...]
    frame[1] = pltpu.roll(tmp[2, 0:rows, :], shift, 1)

    def start_frames(kind):
        for side in range(2):
            side_copy(kind, side).start()
        for vert in range(2):

            @pl.when(senders[vert])
            def _():
                for column in range(3):
                    vert_copy(kind, vert, column).start()

    def wait_frames(kind):
        for side in range(2):
            side_copy(kind, side).wait()
        for vert in range(2):

            @pl.when(senders[vert])
            def _():
                for column in range(3):
                    vert_copy(kind, vert, column).wait_send()

            @pl.when(receivers[vert])
            def _():
                for column in range(3):
                    vert_copy(kind, vert, column).wait_recv()

    start_frames(1)

    halo_columns = ((X0 - HALO, X0), (X0 + span, X0 + span + HALO))

    def put_columns():
        for a in range(2):
            for side, (lo, hi) in enumerate(halo_columns):
                for y in range(BY):
                    strip[a, HALO + y, lo:hi, :] = colrecv[side, a, y]

    def put_corners(vert):
        base = 0 if vert == 0 else HALO + BY
        for a in range(2):
            for side, (lo, hi) in enumerate(halo_columns):
                for y in range(HALO):
                    strip[a, base + y, lo:hi, :] = corner[vert, side, a, y]

    lane = lax.broadcasted_iota(jnp.int32, (8, 128), 1)
    low = lane < HALF
    level = jnp.where(low, lane, lane - HALF).astype(jnp.float32)

    def prepare(tiles, y, depths):
        kept = list(depths)
        for v in tiles:
            here = pl.ds(C0 + 8 * v, 8)
            flow = strip[0, y, here, :]
            depth = jnp.broadcast_to(flow[:, levels : levels + 1], (8, 128))
            mixing = jnp.broadcast_to(flow[:, HALF + levels : HALF + levels + 1], (8, 128))
            turned = pltpu.roll(flow, HALF, 1)
            w_[y, here, :] = jnp.where(level < depth, 1.0, 0.0)
            u_[y, here, :] = jnp.where(low, flow, turned)
            n_[y, here, :] = jnp.where(low, turned, flow)
            m_[y, here, :] = mixing_rate * mixing
            kept[v] = jnp.where(lane == y, depth, depths[v])
        return tuple(kept)

    blank = tuple(jnp.zeros((8, 128), jnp.float32) for _ in range(width_vregs))

    def faces(tiles, y, carry):
        for v in tiles:
            x = C0 + 8 * v
            here = pl.ds(x, 8)
            there = pl.ds(x + 1, 8)
            wet = w_[y, here, :]
            wet_e = wet * w_[y, there, :]
            wet_n = wet * w_[y + 1, here, :]
            we[y, here, :] = wet_e
            wn[y, here, :] = wet_n
            scale = advect_rate * 0.25
            ce[y, here, :] = (scale * wet_e) * (u_[y, here, :] + u_[y, there, :])
            cn[y, here, :] = (scale * wet_n) * (n_[y, here, :] + n_[y + 1, here, :])
        return carry

    def first(f, tiles, y, carry):
        for v in tiles:
            x = C0 + 8 * v
            here, right, left = pl.ds(x, 8), pl.ds(x + 1, 8), pl.ds(x - 1, 8)
            mid = f[y, here, :]
            lap = (
                we[y, here, :] * (f[y, right, :] - mid)
                + we[y, left, :] * (f[y, left, :] - mid)
                + wn[y, here, :] * (f[y + 1, here, :] - mid)
                + wn[y - 1, here, :] * (f[y - 1, here, :] - mid)
            )
            g_[y, here, :] = m_[y, here, :] * lap
        return carry

    def second(f, y, v):
        x = C0 + 8 * v
        here, right, left = pl.ds(x, 8), pl.ds(x + 1, 8), pl.ds(x - 1, 8)
        mid = f[y, here, :]
        gm = g_[y, here, :]
        flow = (
            ce[y, here, :] * (mid + f[y, right, :])
            - ce[y, left, :] * (mid + f[y, left, :])
            + cn[y, here, :] * (mid + f[y + 1, here, :])
            - cn[y - 1, here, :] * (mid + f[y - 1, here, :])
        )
        mix = (
            we[y, here, :] * (g_[y, right, :] - gm)
            + we[y, left, :] * (g_[y, left, :] - gm)
            + wn[y, here, :] * (g_[y + 1, here, :] - gm)
            + wn[y - 1, here, :] * (g_[y - 1, here, :] - gm)
        )
        return mid - (flow + mix)

    old, new = strip.at[1], adv

    def pass_one(tiles, y, carry):
        for v in tiles:
            adv[y, pl.ds(C0 + 8 * v, 8), :] = second(old, y, v)
        return carry

    every = range(width_vregs)

    def early(step, bounds, tiles, carry=0):
        return lax.fori_loop(bounds[0], bounds[1], functools.partial(step, tiles), carry)

    def late(step, outer, bounds, tiles, carry=0):
        rest = [v for v in every if v not in tiles]
        carry = lax.fori_loop(outer[0], bounds[0], functools.partial(step, every), carry)
        carry = lax.fori_loop(bounds[1], outer[1], functools.partial(step, every), carry)
        return lax.fori_loop(bounds[0], bounds[1], functools.partial(step, rest), carry)

    last = rows - HALO
    full = span // 8
    step_one = functools.partial(first, old)
    depth_columns = early(prepare, (HALO, last), range(1, full + 1), blank)
    early(faces, (HALO, last - 1), range(1, full))
    for a in range(2):
        for side in range(2):
            col_copy(a, side).wait()
    for vert in range(2):

        @pl.when(senders[vert])
        def _():
            for side in range(2):
                corner_copy(vert, side).start()

    early(step_one, (HALO + 1, last - 1), range(2, full))
    early(pass_one, (HALO + 2, last - 2), range(3, full - 1))

    for vert in range(2):

        @pl.when(senders[vert])
        def _():
            for a in range(2):
                row_copy(a, vert).wait_send()
            for side in range(2):
                corner_copy(vert, side).wait_send()

        @pl.when(receivers[vert])
        def _():
            for a in range(2):
                row_copy(a, vert).wait_recv()
            for side in range(2):
                corner_copy(vert, side).wait_recv()

    put_columns()
    for vert in range(2):

        @pl.when(receivers[vert])
        def _():
            put_corners(vert)

    depth_columns = late(prepare, (0, rows), (HALO, last), range(1, full + 1), depth_columns)

    lanes = lax.broadcasted_iota(jnp.int32, (rows, 128), 1)
    ys = lax.broadcasted_iota(jnp.int32, (rows, 128), 0)
    sub = lax.broadcasted_iota(jnp.int32, (8, 128), 0)
    inside = (ys >= HALO) & (ys < HALO + BY) & (lanes >= shift) & (lanes < shift + span)

    def nbr_e(v):
        return pltpu.roll(v, 127, 1)

    def nbr_w(v):
        return pltpu.roll(v, 1, 1)

    def nbr_n(v):
        return pltpu.roll(v, rows - 1, 0)

    def nbr_s(v):
        return pltpu.roll(v, 1, 0)

    hops = (nbr_e, nbr_w, nbr_n, nbr_s)

    def to_grid(columns, t):
        for v in range(width_vregs):
            tmp[t, 8 * v : 8 * v + 8, :] = columns[v]
        if width_vregs < 16:
            tmp[t, 8 * width_vregs : 128, :] = jnp.zeros((128 - 8 * width_vregs, 128), jnp.float32)
        return tmp[t].T[0:rows, :]

    def pack(products):
        columns = [jnp.sum(jnp.where(inside, p, 0.0), axis=0, keepdims=True) for p in products]
        row = jnp.zeros((1, 128), jnp.float32)
        place = lax.broadcasted_iota(jnp.int32, (1, 128), 1)
        for k, column in enumerate(columns):
            row = jnp.where(place == k, jnp.sum(column, axis=1, keepdims=True), row)
        return row

    def x_copy(buffer, sems, k):
        return remote(buffer.at[0], buffer.at[k], sems, k, (lax.rem(gx + k, gx_count), gy))

    def y_copy(buffer, sems, k):
        return remote(buffer.at[0], buffer.at[k], sems, k, (gx, lax.rem(gy + k, gy_count)))

    def start_sum(copy, buffer, sems, row):
        buffer[0] = row
        for k in range(1, buffer.shape[0]):
            copy(buffer, sems, k).start()

    def end_sum(copy, buffer, sems):
        for k in range(1, buffer.shape[0]):
            copy(buffer, sems, k).wait()
        total = buffer[0]
        for k in range(1, buffer.shape[0]):
            total = total + buffer[k]
        return total

    depth_grid = to_grid(depth_columns, 1)
    couplings = [jnp.minimum(depth_grid, hop(depth_grid)) / levels for hop in hops]
    coupled = couplings[0] + couplings[1] + couplings[2] + couplings[3]
    squares = sum(c * c for c in couplings)
    own = frame[1] + coupled
    start_sum(
        x_copy, fitx, fitx_sem,
        pack([depth_grid, depth_grid * own, depth_grid * (own * own + squares)]),
    )

    late(faces, (0, rows - 1), (HALO, last - 1), range(1, full))
    late(step_one, (1, rows - 1), (HALO + 1, last - 1), range(2, full))
    late(pass_one, (2, rows - 2), (HALO + 2, last - 2), range(3, full - 1))
    start_sum(y_copy, fity, fity_sem, end_sum(x_copy, fitx, fitx_sem))
    lax.fori_loop(3, rows - 3, functools.partial(first, new, every), 0)
    weight = jnp.where(low, 1.0, -salt_weight) * (1.0 / math.sqrt(levels))

    def pass_two(y, sums):
        kept = []
        for v in range(width_vregs):
            here = pl.ds(C0 + 8 * v, 8)
            value = second(new, y, v)
            strip[1, y, here, :] = value
            total = jnp.sum(w_[y, here, :] * weight * value, axis=1, keepdims=True)
            kept.append(jnp.where(lane == y, jnp.broadcast_to(total, (8, 128)), sums[v]))
        return tuple(kept)

    forcing_columns = lax.fori_loop(HALO, HALO + BY, pass_two, blank)

    frame[0] = to_grid(forcing_columns, 0)
    start_frames(0)

    fit = end_sum(y_copy, fity, fity_sem)
    centre = fit[:, 1:2] / fit[:, 0:1]
    variance = fit[:, 2:3] / fit[:, 0:1] - centre * centre
    spread = jnp.maximum(2.0 * jnp.sqrt(jnp.maximum(variance, 0.0)), 0.1 * centre)
    centre = jnp.broadcast_to(centre, (1, 128))
    spread = jnp.broadcast_to(spread, (1, 128))

    for p in range(slots):
        for y in range(BY):
            cells[p, BX * y : BX * (y + 1), :] = strip[1, HALO + y, X0 + BX * p : X0 + BX * (p + 1), :]

    def give(cols, lanes, base):
        turned = [cells[p, pl.ds(base, 128), :].T for p in range(slots)]
        for s in range(slots):
            for n in range(2):
                value = tr_ref[s, n, :, cols]
                for p in range(slots):
                    piece = turned[p][HALF * n : HALF * n + levels, 0:lanes]
                    value = jnp.where(where_slot[s] == p, piece, value)
                out_v[s, n, :, cols] = value

    def give_chunk(j, carry):
        base = pl.multiple_of(j * 128, 128)
        give(pl.ds(base, 128), 128, base)
        return carry

    lax.fori_loop(0, chunks, give_chunk, 0)
    give(pl.ds(chunks * 128, tail), tail, chunks * 128)
    out_copy = pltpu.make_async_copy(out_v, out_ref, out_sem)
    out_copy.start()

    wait_frames(1)
    wait_frames(0)

    def extended(kind):
        parts = []
        for column, middle in enumerate((sideframe.at[0, kind], frame.at[kind], sideframe.at[1, kind])):
            south = jnp.where(has_s, vertframe[0, column, kind], 0.0)
            north = jnp.where(has_n, vertframe[1, column, kind], 0.0)
            first_rows = jnp.where(sub < HALO, south, middle[0:8, :])
            last_rows = jnp.where(sub < HALO, middle[rows - 8 : rows, :], north)
            parts.append(jnp.concatenate([first_rows, middle[8 : rows - 8, :], last_rows], axis=0))
        return jnp.where(
            lanes < shift,
            pltpu.roll(parts[0], 128 - span, 1),
            jnp.where(lanes < shift + span, parts[1], pltpu.roll(parts[2], span, 1)),
        )

    forcing = extended(0)
    damping = extended(1)

    diagonal = damping + coupled - centre

    def shifted(v):
        beside = [c * hop(v) for c, hop in zip(couplings, hops)]
        return (diagonal * v - (beside[0] + beside[1] + beside[2] + beside[3])) / spread

    basis = [forcing, shifted(forcing)]
    while len(basis) < ITERS + 1:
        basis.append(2.0 * shifted(basis[-1]) - basis[-2])
    pairs = ((0, 0), (0, 1), (1, 1), (1, 2), (2, 2), (2, 3), (0, 2), (0, 3), (1, 3))
    start_sum(x_copy, redx, redx_sem, pack([basis[i] * basis[j] for i, j in pairs]))
    start_sum(y_copy, redy, redy_sem, end_sum(x_copy, redx, redx_sem))
    total = end_sum(y_copy, redy, redy_sem)
    gram = {}
    for k, (i, j) in enumerate(pairs):
        gram[i, j] = gram[j, i] = jnp.broadcast_to(total[:, k : k + 1], (1, 128))

    def inner_product(a, b):
        value = None
        for i, ai in enumerate(a):
            for j, bj in enumerate(b):
                if ai is not None and bj is not None:
                    term = ai * bj * gram[i, j]
                    value = term if value is None else value + term
        return value

    def add(a, b):
        return b if a is None else a if b is None else a + b

    def combine(a, scale, b):
        return [add(ai, None if bi is None else scale * bi) for ai, bi in zip(a, b)]

    def image_of(p):
        image = [None] * (ITERS + 1)
        for i in range(ITERS):
            if p[i] is None:
                continue
            image[i] = add(image[i], centre * p[i])
            if i == 0:
                image[1] = add(image[1], spread * p[i])
            else:
                image[i + 1] = add(image[i + 1], (0.5 * spread) * p[i])
                image[i - 1] = add(image[i - 1], (0.5 * spread) * p[i])
        return image

    one = jnp.ones((1, 128), jnp.float32)
    residual = [one] + [None] * ITERS
    direction = [one] + [None] * ITERS
    height = [None] * (ITERS + 1)
    norm = gram[0, 0]
    for iteration in range(ITERS):
        image = image_of(direction)
        step = norm / inner_product(direction, image)
        height = combine(height, step, direction)
        if iteration + 1 < ITERS:
            residual = combine(residual, -step, image)
            norm_next = inner_product(residual, residual)
            direction = combine(residual, norm_next / norm, direction)
            norm = norm_next
    answer = height[0] * basis[0] + height[1] * basis[1] + height[2] * basis[2]
    answer = pltpu.roll(pltpu.roll(answer, 128 - shift, 1), rows - HALO, 0)
    sh_ref[...] = answer[0:BY, 0:span]
    out_copy.wait()


def per_device(block_list, wet_levels, mixing, velocity, tracers, damping):
    gx_count = lax.axis_size("gx")
    gy_count = lax.axis_size("gy")
    slots = tracers.shape[0]
    span = slots * BX
    rows = BY + 2 * HALO
    wide = -(-(X0 + span + HALO + 8) // 8) * 8
    f32 = jnp.float32
    big = pltpu.VMEM((rows, wide, 128), f32)
    vmem = pl.BlockSpec(memory_space=pltpu.VMEM)
    dma = pltpu.SemaphoreType.DMA
    cell_rows = -(-tracers.shape[3] // 128) * 128
    return pl.pallas_call(
        functools.partial(kernel, gx_count, gy_count),
        out_shape=(
            jax.ShapeDtypeStruct(tracers.shape, f32),
            jax.ShapeDtypeStruct(damping.shape, f32),
        ),
        in_specs=[pl.BlockSpec(memory_space=pltpu.SMEM)] + [vmem] * 5,
        out_specs=(pl.BlockSpec(memory_space=pl.ANY), vmem),
        scratch_shapes=[
            pltpu.VMEM((4, 128, 128), f32),
            pltpu.VMEM((4, cell_rows, 128), f32),
            pltpu.VMEM((2, rows, wide, 128), f32),
            big, big, big, big, big, big, big, big, big, big,
            pltpu.VMEM((2, 2, BY, HALO, 128), f32),
            pltpu.VMEM((2, 2, BY, HALO, 128), f32),
            pltpu.VMEM((2, 2, 2, HALO, HALO, 128), f32),
            pltpu.VMEM((2, rows, 128), f32),
            pltpu.VMEM((2, 2, rows, 128), f32),
            pltpu.VMEM((2, 3, 2, 8, 128), f32),
            pltpu.VMEM((gx_count, 1, 128), f32),
            pltpu.VMEM((gy_count, 1, 128), f32),
            pltpu.VMEM((gx_count, 1, 128), f32),
            pltpu.VMEM((gy_count, 1, 128), f32),
            pltpu.VMEM(tracers.shape, f32),
            dma((2, 4)), dma((2, 4)), dma((2, 4)), dma((2, 4)), dma((2, 12)),
            dma((2, gx_count)), dma((2, gy_count)), dma((2, gx_count)), dma((2, gy_count)), dma,
        ],
        compiler_params=pltpu.CompilerParams(
            collective_id=0, has_side_effects=True, vmem_limit_bytes=62 * 1024 * 1024
        ),
        name="ocean",
    )(block_list, wet_levels, mixing, velocity, tracers, damping)


def solution(mesh):
    return jax.shard_map(
        per_device,
        mesh=mesh,
        in_specs=(
            P(("gx", "gy")),
            P(("gx", "gy"), None),
            P(("gx", "gy"), None),
            P(("gx", "gy"), None, None, None),
            P(("gx", "gy"), None, None, None),
            P("gy", "gx"),
        ),
        out_specs=(P(("gx", "gy"), None, None, None), P("gy", "gx")),
        check_vma=False,
    )
```

time: 61.6 us -> 59.2 us (0.961)
  Pallas kernels: 51.4 us -> 49 us
    pallas_call x1, Pallas kernels: 51.4 us -> 49 us  [per_device(): pl.pallas_call(functools.partial(kernel, gx_count, gy_count), out_shape=(...]
where the time goes in v2:
time: 59.2 us; the launch traced here: 59.1 us
  Pallas kernels  49 us (83%)
  local copies, waits for them, and re-layouts  9.4 us (16%)
  between operations  0.66 us (1%)
    pallas_call x1, Pallas kernels, per_device(): pl.pallas_call(functools.partial(kernel, gx_count, gy_count), out_shape=(...  49 us
    unnamed x7, local copies, waits for them, and re-layouts  5.13 us
    pallas_call x1, local copies, waits for them, and re-layouts, per_device(): pl.pallas_call(functools.partial(kernel, gx_count, gy_count), out_shape=(...  4.27 us

profile of v2, /device:TPU:0, one launch (start us, length us, event | category | flops | bytes accessed | tf_op | source)
XLA Modules:
  0.0 59.1 jit_solution(6093109047445959911)
XLA Ops:
  0.6 0.0 copy-start
  0.6 3.1 %copy.8.vel_ref = f32[2,2,62,1800]{3,2,1,0:T(8,128)} copy(f32[2,2,62,1800]{3,1,2,0:T(2,128)} %param.9) | data formatting | bytes 3571200 | tf_op args[3]
  3.7 0.0 copy-done
  3.7 1.4 %copy.9.tr_ref = f32[2,2,62,1800]{3,2,1,0:T(8,128)} copy(f32[2,2,62,1800]{3,1,2,0:T(2,128)S(1)} %copy-done) | data formatting | bytes 3571200 | tf_op args[4]
  5.2 49.0 %ocean.1 = (f32[2,2,62,1800]{3,2,1,0:T(8,128)}, f32[40,90]{1,0:T(8,128)}) custom-call(s32[2]{0:T(128)} %bl_ref.1, s32[2,1800]{1,0:T(2,128)} %wet_ref.1, f32[2,1800]{1,0:T(2,128)} %mix_ref.1, f32[2,2,62,1800]{3,2,1,0:T(8,128)} %copy.8.vel_ref, f32[2,2,62,1800]{3,2,1,0:T(8,128)} %copy.9.tr_ref, f32[40,90]{1,0:T(8,128)} %damp_ref.1), custom_call_target="tpu_custom_call" | custom-call | tf_op jit(solution)/shard_map/ocean/pallas_call | solution.py:548
  54.2 0.0 copy-start.1
  54.2 4.3 %copy.10 = f32[2,2,62,1800]{3,1,2,0:T(2,128)} copy(f32[2,2,62,1800]{3,2,1,0:T(8,128)} %get-tuple-element.2) | data formatting | bytes 3571200 | tf_op jit(solution)/shard_map/ocean/pallas_call | solution.py:548
  58.4 0.0 copy-done.1
  58.5 0.6 %copy.12 = f32[40,90]{1,0:T(8,128)} copy(f32[40,90]{1,0:T(8,128)S(1)} %copy-done.1) | data formatting | bytes 28800
Async XLA Ops:
  0.6 3.1 %copy-start = (f32[2,2,62,1800]{3,1,2,0:T(2,128)S(1)}, f32[2,2,62,1800]{3,1,2,0:T(2,128)}, u32[]{:S(2)}) copy-start(f32[2,2,62,1800]{3,1,2,0:T(2,128)} %param.10) | copy-start | bytes 5356804
  54.2 4.3 %copy-start.1 = (f32[40,90]{1,0:T(8,128)S(1)}, f32[40,90]{1,0:T(8,128)}, u32[]{:S(2)}) copy-start(f32[40,90]{1,0:T(8,128)} %get-tuple-element.7) | copy-start | bytes 43204

commit v3 on v2

--- a/solution.py
+++ b/solution.py
@@ -573,7 +573,7 @@
             dma((2, gx_count)), dma((2, gy_count)), dma((2, gx_count)), dma((2, gy_count)), dma,
         ],
         compiler_params=pltpu.CompilerParams(
-            collective_id=0, has_side_effects=True, vmem_limit_bytes=62 * 1024 * 1024
+            collective_id=0, has_side_effects=True, vmem_limit_bytes=48 * 1024 * 1024
         ),
         name="ocean",
     )(block_list, wet_levels, mixing, velocity, tracers, damping)

time: 59.2 us -> 53.8 us (0.909)
  local copies, waits for them, and re-layouts: 9.4 us -> 6.15 us
  Pallas kernels: 49 us -> 46.8 us
    pallas_call x1, Pallas kernels: 49 us -> 46.8 us  [per_device(): pl.pallas_call(functools.partial(kernel, gx_count, gy_count), out_shape=(...]
    unnamed x7 -> x13, local copies, waits for them, and re-layouts: 5.13 us -> 3.42 us
    pallas_call x1, local copies, waits for them, and re-layouts: 4.27 us -> 2.72 us  [per_device(): pl.pallas_call(functools.partial(kernel, gx_count, gy_count), out_shape=(...]
where the time goes in v3:
time: 53.8 us; the launch traced here: 53.6 us
  Pallas kernels  46.8 us (87%)
  local copies, waits for them, and re-layouts  6.15 us (11%)
  between operations  0.67 us (1%)
    pallas_call x1, Pallas kernels, per_device(): pl.pallas_call(functools.partial(kernel, gx_count, gy_count), out_shape=(...  46.8 us
    unnamed x13, local copies, waits for them, and re-layouts  3.42 us
    pallas_call x1, local copies, waits for them, and re-layouts, per_device(): pl.pallas_call(functools.partial(kernel, gx_count, gy_count), out_shape=(...  2.72 us

profile of v3, /device:TPU:0, one launch (start us, length us, event | category | flops | bytes accessed | tf_op | source)
XLA Modules:
  0.0 53.6 jit_solution(11227646205194977731)
XLA Ops:
  0.6 0.0 copy-start.4
  0.6 1.8 %copy.8.vel_ref = f32[2,2,62,1800]{3,2,1,0:T(8,128)S(1)} copy(f32[2,2,62,1800]{3,1,2,0:T(2,128)} %param.9) | data formatting | bytes 3571200 | tf_op args[3]
  2.4 0.3 copy-done.4
  2.7 0.0 copy-start
  2.7 0.0 copy-start.1
  2.7 0.0 copy-start.2
  2.7 0.0 copy-start.3
  2.7 0.1 copy.9.tr_ref
  2.9 0.6 %copy-done = f32[40,90]{1,0:T(8,128)S(1)} copy-done((f32[40,90]{1,0:T(8,128)S(1)}, f32[40,90]{1,0:T(8,128)}, u32[]{:S(2)}) %copy-start) | copy-done | bytes 14424
  3.5 0.0 copy-done.1
  3.5 0.0 copy-done.2
  3.5 0.0 copy-done.3
  3.5 46.8 %ocean.1 = (f32[2,2,62,1800]{3,2,1,0:T(8,128)S(1)}, f32[40,90]{1,0:T(8,128)S(1)}) custom-call(s32[2]{0:T(128)S(1)} %copy-done.3, s32[2,1800]{1,0:T(2,128)S(1)} %copy-done.1, f32[2,1800]{1,0:T(2,128)S(1)} %copy-done.2, f32[2,2,62,1800]{3,2,1,0:T(8,128)S(1)} %copy.8.vel_ref, f32[2,2,62,1800]{3,2,1,0:T(8,128)S(1)} %copy.9.tr_ref, f32[40,90]{1,0:T(8,128)S(1)} %copy-done), custom_call_target="tpu_custom_call" | custom-call | tf_op jit(solution)/shard_map/ocean/pallas_call | solution.py:548
  50.2 2.7 %copy.10 = f32[2,2,62,1800]{3,1,2,0:T(2,128)} copy(f32[2,2,62,1800]{3,2,1,0:T(8,128)S(1)} %get-tuple-element.2) | data formatting | bytes 3571200 | tf_op jit(solution)/shard_map/ocean/pallas_call | solution.py:548
  53.0 0.6 %copy.12 = f32[40,90]{1,0:T(8,128)} copy(f32[40,90]{1,0:T(8,128)S(1)} %get-tuple-element.7) | data formatting | bytes 28800
Async XLA Ops:
  0.6 2.1 %copy-start.4 = (f32[2,2,62,1800]{3,1,2,0:T(2,128)S(1)}, f32[2,2,62,1800]{3,1,2,0:T(2,128)}, u32[]{:S(2)}) copy-start(f32[2,2,62,1800]{3,1,2,0:T(2,128)} %param.10) | copy-start | bytes 5356804
  2.7 0.7 %copy-start = (f32[40,90]{1,0:T(8,128)S(1)}, f32[40,90]{1,0:T(8,128)}, u32[]{:S(2)}) copy-start(f32[40,90]{1,0:T(8,128)} %damp_ref.1) | copy-start | bytes 43204
  2.7 0.7 %copy-start.1 = (s32[2,1800]{1,0:T(2,128)S(1)}, s32[2,1800]{1,0:T(2,128)}, u32[]{:S(2)}) copy-start(s32[2,1800]{1,0:T(2,128)} %wet_ref.1) | copy-start | bytes 43204
  2.7 0.7 %copy-start.2 = (f32[2,1800]{1,0:T(2,128)S(1)}, f32[2,1800]{1,0:T(2,128)}, u32[]{:S(2)}) copy-start(f32[2,1800]{1,0:T(2,128)} %mix_ref.1) | copy-start | bytes 43204
  2.7 0.7 %copy-start.3 = (s32[2]{0:T(128)S(1)}, s32[2]{0:T(128)}, u32[]{:S(2)}) copy-start(s32[2]{0:T(128)} %bl_ref.1) | copy-start | bytes 28
